TPU v7x, 32 devices: a 4x4x1 block of a 4x4x8 slice. The times are simulated.
32 devices in a mesh: dp: 1 (over z), sp: 32 (over y, x, core).
Axes of the slice: x: 4, y: 4, z: 1, core: 2. Of those that a mesh axis runs over, the one named last changes fastest.
The devices are a block of a 4x4x8 slice.
Arguments:
- tokens: bfloat16 [128, 4096], P('dp')
- w_query: bfloat16 [4096, 4096], replicated
- w_key: bfloat16 [4096, 128], replicated
- w_value: bfloat16 [4096, 128], replicated
- w_out: bfloat16 [4096, 4096], P('sp')
- k_cache: bfloat16 [128, 8192, 128], P('dp', 'sp')
- v_cache: bfloat16 [128, 8192, 128], P('dp', 'sp')
- positions: int32 [128], P('dp')
Outputs:
- output 1: bfloat16 [128, 4096], P('dp')
- output 2: bfloat16 [128, 8192, 128], P('dp', 'sp')
- output 3: bfloat16 [128, 8192, 128], P('dp', 'sp')
All inputs are finite; a program needn't handle non-finite values.
Results may differ from a plain program's by a relative error of at most 0.00420465.
Values are sent between devices in bfloat16 or wider.
A program may use at most 768 MiB of HBM per device.

v0:
```python
import jax
import jax.numpy as jnp
from jax import lax
from jax.sharding import PartitionSpec as P


def solution(mesh):
    def local_step(tokens, w_query, w_key, w_value, w_out, k_cache, v_cache, positions):
        n_rows, seq_local, head_dim = k_cache.shape
        q_width = w_query.shape[1]
        n_heads = q_width // head_dim
        rows_local = w_out.shape[0]
        shard_idx = lax.axis_index('sp')
        queries = jnp.dot(tokens, w_query, preferred_element_type=jnp.float32).astype(jnp.bfloat16).reshape(n_rows, n_heads, head_dim)
        key_new = jnp.dot(tokens, w_key, preferred_element_type=jnp.float32).astype(jnp.bfloat16)
        value_new = jnp.dot(tokens, w_value, preferred_element_type=jnp.float32).astype(jnp.bfloat16)
        local_pos = positions - shard_idx * seq_local
        slot_ids = jnp.arange(seq_local)
        hit_mask = (slot_ids[None, :] == local_pos[:, None])[:, :, None]
        k_upd = jnp.where(hit_mask, key_new[:, None, :], k_cache)
        v_upd = jnp.where(hit_mask, value_new[:, None, :], v_cache)
        scores = jnp.einsum('bhd,btd->bht', queries, k_upd, preferred_element_type=jnp.float32) * head_dim ** -0.5
        valid_mask = (slot_ids[None, :] <= local_pos[:, None])[:, None, :]
        scores = jnp.where(valid_mask, scores, -jnp.inf)
        row_peak = jnp.maximum(jnp.max(scores, axis=2), -1e30)
        weights = jnp.exp(scores - row_peak[:, :, None])
        weight_sum = jnp.sum(weights, axis=2)
        value_sum = jnp.einsum('bht,btd->bhd', weights.astype(jnp.bfloat16), v_upd, preferred_element_type=jnp.float32)
        peak_all = lax.pmax(row_peak, 'sp')
        rescale = jnp.exp(row_peak - peak_all)
        weight_all = lax.psum(weight_sum * rescale, 'sp')
        value_all = lax.psum(value_sum * rescale[:, :, None], 'sp')
        attn_heads = (value_all / weight_all[:, :, None]).astype(jnp.bfloat16).reshape(n_rows, q_width)
        attn_local = lax.dynamic_slice_in_dim(attn_heads, shard_idx * rows_local, rows_local, axis=1)
        partial = jnp.dot(attn_local, w_out, preferred_element_type=jnp.float32)
        attn_out = lax.psum(partial, 'sp').astype(jnp.bfloat16)
        return attn_out, k_upd, v_upd

    cache_spec = P('dp', 'sp', None)
    return jax.shard_map(local_step, mesh=mesh, in_specs=(P('dp', None), P(), P(), P(), P('sp', None), cache_spec, cache_spec, P('dp')), out_specs=(P('dp', None), cache_spec, cache_spec), check_vma=False)
```

profile of v0, /device:TPU:97, one launch (start us, length us, event | category | flops | bytes accessed | tf_op | source)
XLA Modules:
  0.0 260.3 jit_solution(7569124030278491430)
XLA Ops:
  7.2 0.0 copy-start
  7.2 0.0 copy-start.4
  7.2 0.1 all-reduce.3.cloned.1.call-start
  7.3 1.1 copy-done
  8.4 1.6 convolution_convert_fusion.2
  10.1 1.6 convolution_convert_fusion.1
  11.7 0.0 copy-done.4
  11.7 0.0 slice-start
  11.8 0.1 iota_compare_fusion.1
  11.9 0.0 slice-start.1
  11.9 14.2 %fusion.12 = bf16[16,8,32,128]{3,1,2,0:T(8,128)(2,1)} fusion(bf16[128,4096]{1,0:T(8,128)(2,1)S(1)} %copy-done, bf16[4096,4096]{1,0:T(8,128)(2,1)} %param.9), kind=kOutput, calls=%fused_computation.15 | convolution fusion | flops 4295491584 | bytes 35651584 | tf_op jit(solution)/shard_map/dot_general | solution.py:14
  26.0 1.4 copy.11
  27.5 0.0 slice-done
  27.5 0.0 slice-done.1
  27.5 7.6 %broadcast_select_fusion.1 = (bf16[128,256,128]{2,1,0:T(8,128)(2,1)S(1)}, bf16[128,256,128]{2,1,0:T(8,128)(2,1)}) fusion(bf16[128,256,128]{2,1,0:T(8,128)(2,1)S(1)} %bitcast.18, pred[128,256]{1,0:T(8,128)(4,1)S(1)} %get-tuple-element.8, bf16[128,128]{1,0:T(8,128)(2,1)S(1)} %convolution_convert_fusion.2, bf16[128,256,128]{2,1,0:T(8,128)(2,1)} %param.14, ...), kind=kLoop, calls=%fused_computation.1 | loop fusion | flops 8388608 | bytes 33652736 | tf_op jit(solution)/shard_map/jit(_where)/select_n | solution.py:20
  35.1 0.0 copy-start.3
  35.1 5.0 %fusion = (f32[128,32]{1,0:T(8,128)S(1)}, f32[128,32,256]{2,1,0:T(8,128)}) fusion(pred[128,256]{1,0:T(8,128)(4,1)S(1)} %get-tuple-element.7, bf16[128,32,128]{2,1,0:T(8,128)(2,1)S(1)} %bitcast.20, bf16[128,256,128]{2,1,0:T(8,128)(2,1)S(1)} %get-tuple-element.5), kind=kOutput, calls=%fused_computation.5 | convolution fusion | flops 271577088 | bytes 13680640 | tf_op jit(solution)/shard_map/bhd,btd->bht/dot_general | solution.py:22
  40.1 0.0 copy-done.3
  40.1 50.0 %pmax.7 = f32[128,32]{1,0:T(8,128)S(1)} all-reduce(f32[128,32]{1,0:T(8,128)S(1)} %broadcast_maximum_fusion), channel_id=1, replica_groups=mesh['dp'=1,'sp'=32] {'sp'}, use_global_device_ids=true, to_apply=%region_1.2 | all-reduce | flops 4096 | bytes 32768 | tf_op jit(solution)/shard_map/pmax | solution.py:29
  90.1 0.0 copy-start.2
  90.1 3.4 %fusion.1 = f32[128,32]{1,0:T(8,128)S(1)} fusion(f32[128,32,256]{2,1,0:T(8,128)} %get-tuple-element.10, f32[128,32]{1,0:T(8,128)S(1)} %broadcast_maximum_fusion, pred[128,256]{1,0:T(8,128)(4,1)S(1)} %get-tuple-element.7), kind=kLoop, calls=%fused_computation.6 | loop fusion | flops 4190208 | bytes 4259840 | tf_op jit(solution)/shard_map/reduce_sum | solution.py:27
  93.5 0.0 copy-done.2
  93.6 5.6 %fusion.9 = f32[128,32,128]{2,1,0:T(8,128)} fusion(bf16[128,256,128]{2,1,0:T(8,128)(2,1)} %get-tuple-element.6, f32[128,32,256]{2,1,0:T(8,128)S(1)} %copy-done.2, f32[128,32]{1,0:T(8,128)S(1)} %broadcast_maximum_fusion, pred[128,256]{1,0:T(8,128)(4,1)S(1)} %get-tuple-element.7, f32[128,32]{1,0:T(8,128)S(1)} %get-tuple-element.4), kind=kOutput, calls=%fused_computation.14 | convolution fusion | flops 273154048 | bytes 14745600 | tf_op jit(solution)/shard_map/bht,btd->bhd/dot_general | solution.py:28
  99.1 0.1 all-reduce.3.cloned.1.call-update
  99.2 43.9 %psum.22 = f32[128,32]{1,0:T(8,128)S(1)} all-reduce(f32[128,32]{1,0:T(8,128)S(1)} %get-tuple-element.3), channel_id=1, replica_groups=mesh['dp'=1,'sp'=32] {'sp'}, use_global_device_ids=true, to_apply=%region_4.5 | all-reduce | flops 4096 | bytes 32768 | tf_op jit(solution)/shard_map/psum | solution.py:31
  143.1 52.0 %all-reduce.3.cloned.1.call-done = f32[128,32,128]{2,1,0:T(8,128)} async-done(((f32[128,32,128]{2,1,0:T(8,128)}), f32[128,32,128]{2,1,0:T(8,128)}) %all-reduce.3.cloned.1.call-update) | async-done | bytes 2097168 | tf_op jit(solution)/shard_map/psum | solution.py:32
  195.1 1.9 divide_convert_fusion
  197.1 0.0 copy-start.1
  197.1 0.5 copy.14
  197.5 1.7 fusion.13
  199.2 54.2 %all-reduce.4 = bf16[128,4096]{1,0:T(8,128)(2,1)} all-reduce(f32[128,4096]{1,0:T(8,128)S(1)} %fusion.13), channel_id=1, replica_groups=mesh['dp'=1,'sp'=32] {'sp'}, use_global_device_ids=true, to_apply=%region_5.6 | all-reduce | flops 524288 | bytes 3145728 | tf_op jit(solution)/shard_map/psum | solution.py:36
  253.4 0.0 copy-done.1
  (4 shorter events, 0.0 us)
Async XLA Ops:
  7.2 1.2 copy-start
  7.2 4.5 %copy-start.4 = (s32[128]{0:T(128)S(1)}, s32[128]{0:T(128)}, u32[]{:S(2)}) copy-start(s32[128]{0:T(128)} %param.15) | copy-start | bytes 1540
  7.2 187.9 %all-reduce.3.cloned.1.call-start = ((), (), s32[]{:S(2)}) async-start(), calls=%async_computation | async-start | bytes 4194304 | tf_op jit(solution)/shard_map/psum | solution.py:32
  11.7 15.7 %slice-start = ((s8[8388608]{0:T(1024)(128)(4,1)}), s8[4194304]{0:T(1024)(128)(4,1)S(1)}, s32[]{:S(2)}) async-start(s8[8388608]{0:T(1024)(128)(4,1)} %bitcast.17), calls=%async_computation.1 | async-start | bytes 8388608
  11.9 15.6 %slice-start.1 = ((s8[8388608]{0:T(1024)(128)(4,1)}), s8[4194304]{0:T(1024)(128)(4,1)S(1)}, s32[]{:S(2)}) async-start(s8[8388608]{0:T(1024)(128)(4,1)} %bitcast.17), calls=%async_computation.2 | async-start | bytes 8388608
  35.1 5.0 %copy-start.3 = (bf16[128,256,128]{2,1,0:T(8,128)(2,1)}, bf16[128,256,128]{2,1,0:T(8,128)(2,1)S(1)}, u32[]{:S(2)}) copy-start(bf16[128,256,128]{2,1,0:T(8,128)(2,1)S(1)} %get-tuple-element.5) | copy-start | bytes 25165828
  90.1 3.4 %copy-start.2 = (f32[128,32,256]{2,1,0:T(8,128)S(1)}, f32[128,32,256]{2,1,0:T(8,128)}, u32[]{:S(2)}) copy-start(f32[128,32,256]{2,1,0:T(8,128)} %get-tuple-element.10) | copy-start | bytes 12582916
  197.1 56.3 %copy-start.1 = (bf16[128,4096]{1,0:T(8,128)(2,1)S(1)}, bf16[128,4096]{1,0:T(8,128)(2,1)}, u32[]{:S(2)}) copy-start(bf16[128,4096]{1,0:T(8,128)(2,1)} %param.8) | copy-start | bytes 3145732
Sparse Core Ops, SparseCore 0:
  99.3 95.7 all-reduce.2
where the time goes:
time: 261 us; the launch traced here: 260 us
  blocking collectives  148 us (57%)
  waiting for transfers between devices  52.1 us (20%)
  matrix products  29.7 us (11%)
  between operations  14.2 us (5%)
  other arithmetic  13.1 us (5%)
  local copies, waits for them, and re-layouts  3.1 us (1%)
    psum x1, blocking collectives, local_step(): attn_out = lax.psum(partial, 'sp').astype(jnp.bfloat16)  54.2 us
    psum x1, waiting for transfers between devices, local_step(): value_all = lax.psum(value_sum * rescale[:, :, None], 'sp')  52 us
    pmax x1, blocking collectives, local_step(): peak_all = lax.pmax(row_peak, 'sp')  50 us
    psum x1, blocking collectives, local_step(): weight_all = lax.psum(weight_sum * rescale, 'sp')  43.9 us
    dot_general x1, matrix products, local_step(): jnp.dot(tokens, w_query, preferred_element_type=jnp.float32)  14.2 us
    select_n x1, other arithmetic, local_step(): k_upd = jnp.where(hit_mask, key_new[:, None, :], k_cache)  7.63 us
    dot_general x1, matrix products, local_step(): jnp.einsum('bht,btd->bhd', weights.astype(jnp.bfloat16), v_upd, preferred...  5.58 us
  transfers between devices with their start and end apart: 1, of which 1 were waited for; matrix products, arithmetic and copies ran while one was open for 0% of the time, Pallas kernels for 0%

commit v1 on v0

v1 whole, which is shorter than its diff:
```python
import functools
import math

import jax
import jax.numpy as jnp
from jax import lax
from jax.experimental import pallas as pl
from jax.experimental.pallas import tpu as pltpu
from jax.sharding import PartitionSpec as P

MESH = pl.DeviceIdType.MESH
BF16, F32 = jnp.bfloat16, jnp.float32
LOWEST = -3.0e38


class Grid:
    def __init__(self, n):
        self.n = n
        self.a = a = math.isqrt(n // 2)
        me = lax.axis_index('sp')
        self.me = me
        self.c = lax.rem(me, 2)
        self.x = lax.rem(me // 2, a)
        self.y = me // (2 * a)

    def index(self, y, x, c):
        return (y * self.a + x) * 2 + c

    def y_at(self, r):
        return lax.rem(self.y + r, self.a)

    def x_at(self, r):
        return lax.rem(self.x + r, self.a)

    def y_peer(self, r):
        return self.index(self.y_at(r), self.x, self.c)

    def x_peer(self, r):
        return self.index(self.y, self.x_at(r), self.c)

    def partner(self):
        return self.index(self.y, self.x, 1 - self.c)

    def peers(self):
        out = [self.partner()]
        for r in range(1, self.a):
            out += [self.y_peer(r), self.x_peer(r)]
        return out

    def greet(self):
        barrier = pltpu.get_barrier_semaphore()
        for p in self.peers():
            pl.semaphore_signal(barrier, inc=1, device_id={'sp': p}, device_id_type=MESH)

    def greeted(self):
        pl.semaphore_wait(pltpu.get_barrier_semaphore(), 2 * self.a - 1)


def remote(src, dst, send, recv, dev):
    return pltpu.make_async_remote_copy(src_ref=src, dst_ref=dst, send_sem=send, recv_sem=recv, device_id={'sp': dev}, device_id_type=MESH)


class Gather:
    def __init__(self, g, buf, send, recv):
        self.g, self.buf, self.send, self.recv = g, buf, send, recv
        rows = buf.shape[3]
        self.lo, self.hi = pl.ds(0, rows // 2), pl.ds(rows // 2, rows // 2)

    def ring_copies(self, first):
        g, buf, a = self.g, self.buf, self.g.a
        out = []
        for r in range(1, a):
            if first:
                srcs = (buf.at[g.y, g.x, g.c, self.lo], buf.at[g.y, g.x, g.c, self.hi])
            else:
                srcs = (buf.at[:, g.x, g.c, self.lo], buf.at[g.y, :, g.c, self.hi])
            peers = (g.y_peer(r), g.x_peer(r)) if first else (g.x_peer(r), g.y_peer(r))
            for i in range(2):
                k = ((0 if first else 2) + i) * (a - 1) + r - 1
                out.append(remote(srcs[i], srcs[i], self.send.at[k], self.recv.at[k], peers[i]))
        return out

    def start(self):
        self.first = self.ring_copies(True)
        for cp in self.first:
            cp.start()

    def finish(self):
        g, buf = self.g, self.buf
        for cp in self.first:
            cp.wait_recv()
        second = self.ring_copies(False)
        for cp in second:
            cp.start()
        for cp in second:
            cp.wait_recv()
        k = 4 * (g.a - 1)
        plane = buf.at[:, :, g.c]
        last = remote(plane, plane, self.send.at[k], self.recv.at[k], g.partner())
        last.start()
        last.wait_recv()
        for cp in self.first + second + [last]:
            cp.wait_send()

    @staticmethod
    def sems(a):
        return 4 * (a - 1) + 1


def project_kernel(n, x_hbm, wq_hbm, wk_hbm, wv_hbm, q_out, kv_out, xv, wqv, wkv, lsem, send, recv):
    g = Grid(n)
    hd = wqv.shape[1]
    col = pl.multiple_of(g.me * hd, hd)
    copies = [
        pltpu.make_async_copy(x_hbm, xv, lsem.at[0]),
        pltpu.make_async_copy(wq_hbm.at[:, pl.ds(col, hd)], wqv, lsem.at[1]),
        pltpu.make_async_copy(wk_hbm, wkv.at[:, pl.ds(0, hd)], lsem.at[2]),
        pltpu.make_async_copy(wv_hbm, wkv.at[:, pl.ds(hd, hd)], lsem.at[3]),
    ]
    for cp in copies:
        cp.start()
    g.greet()
    copies[0].wait()
    copies[1].wait()
    q = jnp.dot(xv[...], wqv[...], preferred_element_type=F32).astype(BF16)
    q_out[g.y, g.x, g.c] = q
    g.greeted()
    gather = Gather(g, q_out, send, recv)
    gather.start()
    copies[2].wait()
    copies[3].wait()
    kv = jnp.dot(xv[...], wkv[...], preferred_element_type=F32).astype(BF16)
    kv_out[0] = kv[:, :hd].astype(F32)
    kv_out[1] = kv[:, hd:].astype(F32)
    gather.finish()


def attend_kernel(blk, pos, q_ref, kv_new, k_hbm, v_hbm, ko_hbm, vo_hbm, o_ref, ml_ref, kbuf, vbuf, q32, rsem, wsem):
    n_rows, t_loc, hd = kbuf.shape
    n_heads = o_ref.shape[0] // n_rows
    n_blk = n_rows // blk
    base = lax.axis_index('sp') * t_loc
    scale = hd ** -0.5 * math.log2(math.e)

    def reads(i):
        rows = pl.ds(i * blk, blk)
        return (pltpu.make_async_copy(k_hbm.at[rows], kbuf.at[rows], rsem.at[0, i]), pltpu.make_async_copy(v_hbm.at[rows], vbuf.at[rows], rsem.at[1, i]))

    def writes(i):
        rows = pl.ds(i * blk, blk)
        return (pltpu.make_async_copy(kbuf.at[rows], ko_hbm.at[rows], wsem.at[0, i]), pltpu.make_async_copy(vbuf.at[rows], vo_hbm.at[rows], wsem.at[1, i]))

    @pl.loop(0, n_blk)
    def _(i):
        for cp in reads(i):
            cp.start()

    @pl.loop(0, n_heads)
    def _(h):
        q32[pl.ds(h * n_rows, n_rows), :] = q_ref[h].astype(F32)

    ml_ref[...] = jnp.zeros_like(ml_ref)
    lane = lax.broadcasted_iota(jnp.int32, (n_heads, t_loc), 1)
    lane_b = lax.broadcasted_iota(jnp.int32, (n_heads, n_rows), 1)
    tile_row = lax.broadcasted_iota(jnp.int32, (16, hd), 0)

    @pl.loop(0, n_blk)
    def _(i):
        for cp in reads(i):
            cp.wait()
        slots = []
        for u in range(blk):
            b = i * blk + u
            p = pos[b] - base
            slots.append((b, p))
            t0 = pl.multiple_of(jnp.clip(p, 0, t_loc - 1) // 16 * 16, 16)
            hit = tile_row == p - t0
            for which, buf in enumerate((kbuf, vbuf)):
                new = jnp.broadcast_to(kv_new[which, pl.ds(b, 1), :], (16, hd))
                old = buf[b, pl.ds(t0, 16), :].astype(F32)
                buf[b, pl.ds(t0, 16), :] = jnp.where(hit, new, old).astype(BF16)
        for cp in writes(i):
            cp.start()
        m_acc, l_acc = ml_ref[0], ml_ref[1]
        for b, p in slots:
            qb = q32[pl.ds(b, n_heads, stride=n_rows), :].astype(BF16)
            s = lax.dot_general(qb, kbuf[b], (((1,), (1,)), ((), ())), preferred_element_type=F32) * scale
            s = jnp.where(lane <= p, s, -jnp.inf)
            m = jnp.maximum(jnp.max(s, axis=1, keepdims=True), LOWEST)
            w = jnp.exp2(s - m)
            l = jnp.sum(w, axis=1, keepdims=True)
            o = jnp.dot(w.astype(BF16), vbuf[b], preferred_element_type=F32)
            o_ref[pl.ds(b, n_heads, stride=n_rows), :] = o
            m_acc = jnp.where(lane_b == b, m, m_acc)
            l_acc = jnp.where(lane_b == b, l, l_acc)
        ml_ref[0] = m_acc
        ml_ref[1] = l_acc

    @pl.loop(0, n_blk)
    def _(i):
        for cp in writes(i):
            cp.wait()


def merge(ms, ls):
    top = functools.reduce(jnp.maximum, ms)
    fs = [jnp.exp2(m - top) for m in ms]
    total = functools.reduce(jnp.add, [l * f for l, f in zip(ls, fs)])
    return top, fs, total


def combine_kernel(n, o_ref, ml_ref, wo_ref, y_out, r0, ml0, rows, fa, fb, fcol, mla, mlb, r1a, r1b, rmla, rmlb, s2a, s2b, sm2a, sm2b, r2a, r2b, rm2a, rm2b, go, send0, recv0, send1, recv1, send2, recv2, asend, arecv, bsend, brecv):
    g = Grid(n)
    a = g.a
    n_rows, hd = o_ref.shape[3:]
    half = n_rows // 2
    lo, hi = pl.ds(0, half), pl.ds(half, half)
    g.greet()
    g.greeted()
    order = sorted(range(a - 1), key=lambda r: -min(r + 1, a - 1 - r)) + [a - 1]

    ml_cp = remote(ml_ref, ml0, send0.at[2 * a], recv0.at[2 * a], g.partner())
    ml_cp.start()
    core_a, core_b = {}, {}
    for r in order:
        hy, hx = g.y_at(r + 1), g.x_at(r + 1)
        core_a[r] = remote(o_ref.at[hy, :, 1 - g.c, lo], r0.at[hy, :, lo], send0.at[r], recv0.at[r], g.partner())
        core_b[r] = remote(o_ref.at[:, hx, 1 - g.c, hi], r0.at[:, hx, hi], send0.at[a + r], recv0.at[a + r], g.partner())
        core_a[r].start()
        core_b[r].start()
    ml_cp.wait_recv()
    own = pl.ds(g.c, a * a, stride=2)
    top, fs, total = merge([ml_ref[0, own, :], ml0[0, own, :]], [ml_ref[1, own, :], ml0[1, own, :]])
    for i, v in enumerate([top, total] + fs):
        rows[i] = v
    for i in range(a):
        for k, (da, db) in enumerate(((mla, mlb), (mla, mlb), (fa, fb), (fa, fb))):
            dst = pl.ds(k % 2 * a, a)
            da[i, dst, :] = rows[k, pl.ds(i * a, a), :]
            db[i, dst, :] = rows[k, pl.ds(i, a, stride=a), :]

    ring1 = []
    for r in order:
        hy, hx = g.y_at(r + 1), g.x_at(r + 1)
        core_a[r].wait_recv()
        ft = fa[hy].T[:half]
        for j in range(a):
            r0[hy, j, lo] = o_ref[hy, j, g.c, lo] * ft[:, j:j + 1] + r0[hy, j, lo] * ft[:, a + j:a + j + 1]
        if r < a - 1:
            ring1 += [
                remote(mla.at[hy], rmla.at[r], send1.at[0, r], recv1.at[0, r], g.y_peer(r + 1)),
                remote(r0.at[hy, :, lo], r1a.at[r], send1.at[1, r], recv1.at[1, r], g.y_peer(r + 1)),
            ]
            ring1[-2].start()
            ring1[-1].start()
        core_b[r].wait_recv()
        ft = fb[hx].T[half:]
        for j in range(a):
            r0[j, hx, hi] = o_ref[j, hx, g.c, hi] * ft[:, j:j + 1] + r0[j, hx, hi] * ft[:, a + j:a + j + 1]
        if r < a - 1:
            ring1 += [
                remote(mlb.at[hx], rmlb.at[r], send1.at[2, r], recv1.at[2, r], g.x_peer(r + 1)),
                remote(r0.at[:, hx, hi], r1b.at[r], send1.at[3, r], recv1.at[3, r], g.x_peer(r + 1)),
            ]
            ring1[-2].start()
            ring1[-1].start()
    for cp in ring1:
        cp.wait_recv()

    for side, (ml_own, ml_got, dst, sm) in enumerate(((mla, rmla, s2a, sm2a), (mlb, rmlb, s2b, sm2b))):
        place = g.x if side else g.y
        parts = [ml_own.at[place]] + [ml_got.at[r] for r in range(a - 1)]
        top, fs, total = merge([p[pl.ds(0, a), :] for p in parts], [p[pl.ds(a, a), :] for p in parts])
        for s in range(a):
            fcol[pl.ds(s * a, a), :] = fs[s]
        rows[0, pl.ds(0, a), :] = top
        rows[1, pl.ds(0, a), :] = total
        ft = fcol[...].T[half * side:half * (side + 1)]
        for j in range(a):
            sm[j, 0:1, :] = rows[0, j:j + 1, :]
            sm[j, 1:2, :] = rows[1, j:j + 1, :]
            acc = (r0[j, g.x, hi] if side else r0[g.y, j, lo]) * ft[:, j:j + 1]
            for r in range(a - 1):
                got = r1b[r, j] if side else r1a[r, j]
                acc = acc + got * ft[:, (r + 1) * a + j:(r + 1) * a + j + 1]
            dst[j] = acc

    ring2 = []
    for r in order[:-1]:
        hy, hx = g.y_at(r + 1), g.x_at(r + 1)
        ring2 += [
            remote(sm2a.at[hx], rm2a.at[r], send2.at[0, r], recv2.at[0, r], g.x_peer(r + 1)),
            remote(s2a.at[hx], r2a.at[r], send2.at[1, r], recv2.at[1, r], g.x_peer(r + 1)),
            remote(sm2b.at[hy], rm2b.at[r], send2.at[2, r], recv2.at[2, r], g.y_peer(r + 1)),
            remote(s2b.at[hy], r2b.at[r], send2.at[3, r], recv2.at[3, r], g.y_peer(r + 1)),
        ]
    for cp in ring2:
        cp.start()
    for cp in ring2:
        cp.wait_recv()
    for side, (sm, rm, mine, got) in enumerate(((sm2a, rm2a, s2a, r2a), (sm2b, rm2b, s2b, r2b))):
        place = g.y if side else g.x
        parts = [sm.at[place]] + [rm.at[r] for r in range(a - 1)]
        top, fs, total = merge([p[0:1, :] for p in parts], [p[1:2, :] for p in parts])
        for s in range(a):
            fcol[pl.ds(s, 1), :] = fs[s]
        fcol[pl.ds(a, 1), :] = total
        ft = fcol[...].T[half * side:half * (side + 1)]
        acc = mine[place] * ft[:, 0:1]
        for r in range(a - 1):
            acc = acc + got[r] * ft[:, r + 1:r + 2]
        go[g.y, g.x, g.c, (hi if side else lo), :] = (acc / ft[:, a:a + 1]).astype(BF16)

    heads = Gather(g, go, asend, arecv)
    heads.start()
    heads.finish()
    acc = jnp.zeros((n_rows, wo_ref.shape[1]), F32)
    for k in range(a * a):
        lhs = jnp.concatenate([go[k // a, k % a, 0], go[k // a, k % a, 1]], axis=1)
        acc = acc + jnp.dot(lhs, wo_ref[pl.ds(k * 2 * hd, 2 * hd), :], preferred_element_type=F32)
    y_out[g.y, g.x, g.c] = acc.astype(BF16)
    outs = Gather(g, y_out, bsend, brecv)
    outs.start()
    outs.finish()
    for cp in [ml_cp] + list(core_a.values()) + list(core_b.values()) + ring1 + ring2:
        cp.wait_send()


def solution(mesh):
    n = mesh.shape['sp']
    a = math.isqrt(n // 2)
    vmem, hbm, smem = (pl.BlockSpec(memory_space=s) for s in (pltpu.VMEM, pltpu.HBM, pltpu.SMEM))
    dma = pltpu.SemaphoreType.DMA

    def local_step(tokens, w_query, w_key, w_value, w_out, k_cache, v_cache, positions):
        n_rows, t_loc, hd = k_cache.shape
        d_model = tokens.shape[1]
        wo = lax.all_to_all(w_out.reshape(w_out.shape[0], n, -1), 'sp', split_axis=1, concat_axis=0, tiled=True)
        wo = wo.reshape(w_out.shape[0] * n, -1)
        half = n_rows // 2
        sems = [dma((Gather.sems(a),))] * 2
        q_all, kv_new = pl.pallas_call(
            functools.partial(project_kernel, n),
            out_shape=(jax.ShapeDtypeStruct((a, a, 2, n_rows, hd), BF16), jax.ShapeDtypeStruct((2, n_rows, hd), F32)),
            in_specs=[hbm] * 4,
            out_specs=(vmem, vmem),
            scratch_shapes=[pltpu.VMEM((n_rows, d_model), BF16), pltpu.VMEM((d_model, hd), BF16), pltpu.VMEM((d_model, 2 * hd), BF16), dma((4,))] + sems,
            compiler_params=pltpu.CompilerParams(collective_id=0, has_side_effects=True, vmem_limit_bytes=10 << 20),
            name='project',
        )(tokens, w_query, w_key, w_value)
        blk = 8
        cache = jax.ShapeDtypeStruct(k_cache.shape, k_cache.dtype)
        k_upd, v_upd, o, ml = pl.pallas_call(
            functools.partial(attend_kernel, blk),
            out_shape=(cache, cache, jax.ShapeDtypeStruct((n * n_rows, hd), F32), jax.ShapeDtypeStruct((2, n, n_rows), F32)),
            in_specs=[smem, vmem, vmem, hbm, hbm],
            out_specs=(hbm, hbm, vmem, vmem),
            scratch_shapes=[pltpu.VMEM(k_cache.shape, BF16)] * 2 + [pltpu.VMEM((n * n_rows, hd), F32)] + [dma((2, n_rows // blk))] * 2,
            compiler_params=pltpu.CompilerParams(vmem_limit_bytes=28 << 20),
            name='attend',
        )(positions, q_all.reshape(n, n_rows, hd), kv_new, k_cache, v_cache)
        f32 = lambda *s: pltpu.VMEM(s, F32)
        y = pl.pallas_call(
            functools.partial(combine_kernel, n),
            out_shape=jax.ShapeDtypeStruct((a, a, 2, n_rows, w_out.shape[1] // n), BF16),
            in_specs=[vmem] * 3,
            out_specs=vmem,
            scratch_shapes=[f32(a, a, n_rows, hd), f32(2, n, n_rows), f32(4, a * a, n_rows)]
            + [f32(a, 2 * a, n_rows)] * 2 + [f32(max(a * a, 8), n_rows)] + [f32(a, 2 * a, n_rows)] * 2
            + [f32(a - 1, a, half, hd)] * 2 + [f32(a - 1, 2 * a, n_rows)] * 2
            + [f32(a, half, hd)] * 2 + [f32(a, 8, n_rows)] * 2 + [f32(a - 1, half, hd)] * 2 + [f32(a - 1, 8, n_rows)] * 2
            + [pltpu.VMEM((a, a, 2, n_rows, hd), BF16)]
            + [dma((2 * a + 1,))] * 2 + [dma((4, a - 1))] * 4 + sems * 2,
            compiler_params=pltpu.CompilerParams(collective_id=1, has_side_effects=True, vmem_limit_bytes=14 << 20),
            name='combine',
        )(o.reshape(a, a, 2, n_rows, hd), ml, wo)
        y = y.reshape(n, n_rows, -1).transpose(1, 0, 2).reshape(n_rows, -1)
        return y, k_upd, v_upd

    cache_spec = P('dp', 'sp', None)
    return jax.shard_map(local_step, mesh=mesh, in_specs=(P('dp', None), P(), P(), P(), P('sp', None), cache_spec, cache_spec, P('dp')), out_specs=(P('dp', None), cache_spec, cache_spec), check_vma=False)
```

time: 261 us -> 126 us (0.48)
  blocking collectives: 148 us -> 0 us
  Pallas kernels: 0 us -> 91.3 us
  waiting for transfers between devices: 52.1 us -> 0.01 us
  matrix products: 29.7 us -> 0 us
  local copies, waits for them, and re-layouts: 3.1 us -> 24.3 us
  between operations: 14.2 us -> 0.73 us
  other arithmetic: 13.1 us -> 0 us
  starting transfers between devices: 0.06 us -> 9.14 us
    psum x2 -> x0, blocking collectives: 98.1 us -> none  [the longest x1 54.2 us: local_step(): attn_out = lax.psum(partial, 'sp').astype(jnp.bfloat16)]
    pallas_call x0 -> x3, Pallas kernels: none -> 91.3 us  [the longest x1 39.8 us: local_step(): pl.pallas_call(functools.partial(combine_kernel, n), out_shape=jax.ShapeD...]
    psum x1 -> x0, waiting for transfers between devices: 52 us -> none  [local_step(): value_all = lax.psum(value_sum * rescale[:, :, None], 'sp')]
    pmax x1 -> x0, blocking collectives: 50 us -> none  [local_step(): peak_all = lax.pmax(row_peak, 'sp')]
    dot_general x6 -> x0, matrix products: 29.7 us -> none  [the longest x1 14.2 us: local_step(): jnp.dot(tokens, w_query, preferred_element_type=jnp.float32)]
    unnamed x16 -> x22, local copies, waits for them, and re-layouts: 3.1 us -> 21.8 us
    all_to_all x0 -> x1, starting transfers between devices: none -> 9.14 us  [local_step(): lax.all_to_all(w_out.reshape(w_out.shape[0], n, -1), 'sp', split_axis=1,...]
    select_n x1 -> x0, other arithmetic: 7.63 us -> none  [local_step(): k_upd = jnp.where(hit_mask, key_new[:, None, :], k_cache)]
  transfers between devices with their start and end apart: 1 -> 1, of which waited for: 1 -> 0; matrix products, arithmetic and copies ran while one was open for 0% -> 0% of each run, Pallas kernels for 0% -> 41%
where the time goes in v1:
time: 126 us; the launch traced here: 125 us
  Pallas kernels  91.3 us (72%)
  local copies, waits for them, and re-layouts  24.3 us (19%)
  starting transfers between devices  9.14 us (7%)
    pallas_call x1, Pallas kernels, local_step(): pl.pallas_call(functools.partial(combine_kernel, n), out_shape=jax.ShapeD...  39.8 us
    pallas_call x1, Pallas kernels, local_step(): pl.pallas_call(functools.partial(attend_kernel, blk), out_shape=(cache, c...  36.1 us
    unnamed x22, local copies, waits for them, and re-layouts  21.8 us
    pallas_call x1, Pallas kernels, local_step(): pl.pallas_call(functools.partial(project_kernel, n), out_shape=(jax.Shape...  15.3 us
    all_to_all x1, starting transfers between devices, local_step(): lax.all_to_all(w_out.reshape(w_out.shape[0], n, -1), 'sp', split_axis=1,...  9.14 us
  transfers between devices with their start and end apart: 1, of which 0 were waited for; matrix products, arithmetic and copies ran while one was open for 0% of the time, Pallas kernels for 41%

profile of v1, /device:TPU:97, one launch (start us, length us, event | category | flops | bytes accessed | tf_op | source)
XLA Modules:
  0.0 125.5 jit_solution(9477844434811863387)
XLA Ops:
  0.6 0.0 copy-start
  0.6 1.2 copy-done
  1.9 1.3 %copy_bitcast_fusion.1 = bf16[128,32,128]{2,0,1:T(8,128)(2,1)} fusion(bf16[128,4096]{1,0:T(8,128)(2,1)S(1)} %copy-done), kind=kLoop, calls=%fused_computation.1 | loop fusion | bytes 2097152 | tf_op jit(solution)/shard_map/reshape | solution.py:338
  3.1 9.1 %all-to-all-start = ((bf16[128,32,128]{2,0,1:T(8,128)(2,1)}), bf16[128,32,128]{2,0,1:T(8,128)(2,1)S(1)}, u32[]{:S(2)}, u32[]{:S(2)}) async-start(bf16[128,32,128]{2,0,1:T(8,128)(2,1)} %copy_bitcast_fusion.1), calls=%async_computation | async-start | bytes 2097152 | tf_op jit(solution)/shard_map/all_to_all | solution.py:338
  12.3 0.0 copy-start.2
  12.3 10.5 %copy-done.2 = bf16[4096,4096]{1,0:T(8,128)(2,1)S(1)} copy-done((bf16[4096,4096]{1,0:T(8,128)(2,1)S(1)}, bf16[4096,4096]{1,0:T(8,128)(2,1)}, u32[]{:S(2)}) %copy-start.2) | copy-done | bytes 33554456
  22.8 0.0 copy-start.7
  22.8 1.2 copy-done.7
  24.0 0.0 copy-start.8
  24.0 1.2 copy-done.8
  25.3 0.0 copy-start.9
  25.3 1.2 copy-done.9
  26.5 0.0 copy-start.3
  26.5 0.0 copy-start.10
  26.5 15.3 %project.1 = (bf16[4,4,2,128,128]{4,3,2,1,0:T(8,128)(2,1)S(1)}, f32[2,128,128]{2,1,0:T(8,128)S(1)}) custom-call(bf16[128,4096]{1,0:T(8,128)(2,1)S(1)} %copy-done.7, bf16[4096,4096]{1,0:T(8,128)(2,1)S(1)} %copy-done.2, bf16[4096,128]{1,0:T(8,128)(2,1)S(1)} %copy-done.8, bf16[4096,128]{1,0:T(8,128)(2,1)S(1)} %copy-done.9), custom_call_target="tpu_custom_call" | custom-call | tf_op jit(solution)/shard_map/project/pallas_call | solution.py:342
  41.8 0.0 copy-start.1
  41.8 0.0 copy-done.3
  41.8 0.0 copy-done.10
  41.8 0.0 copy-start.4
  41.8 3.5 %copy-done.4 = bf16[128,256,128]{2,1,0:T(8,128)(2,1)S(1)} copy-done((bf16[128,256,128]{2,1,0:T(8,128)(2,1)S(1)}, bf16[128,256,128]{2,1,0:T(8,128)(2,1)}, u32[]{:S(2)}) %copy-start.4) | copy-done | bytes 8388632
  45.3 36.1 %attend.1 = (bf16[128,256,128]{2,1,0:T(8,128)(2,1)}, bf16[128,256,128]{2,1,0:T(8,128)(2,1)}, f32[4096,128]{1,0:T(8,128)S(1)}, f32[2,32,128]{2,1,0:T(8,128)S(1)}) custom-call(s32[128]{0:T(128)S(1)} %copy-done.10, bf16[32,128,128]{2,1,0:T(8,128)(2,1)S(1)} %bitcast.22, f32[2,128,128]{2,1,0:T(8,128)S(1)} %get-tuple-element.10.kv_new, ...), custom_call_target="tpu_custom_call" | custom-call | tf_op jit(solution)/shard_map/attend/pallas_call | solution.py:353
  81.4 0.0 copy-start.5
  81.4 1.3 %copy-done.5 = f32[4096,128]{1,0:T(8,128)} copy-done((f32[4096,128]{1,0:T(8,128)}, f32[4096,128]{1,0:T(8,128)S(1)}, u32[]{:S(2)}) %copy-start.5) | copy-done | bytes 2097176
  82.8 0.0 all-to-all-done
  82.8 0.0 copy-start.6
  82.8 1.6 %copy-done.6 = f32[4096,128]{1,0:T(8,128)S(1)} copy-done((f32[4096,128]{1,0:T(8,128)S(1)}, f32[4096,128]{1,0:T(8,128)}, u32[]{:S(2)}) %copy-start.6) | copy-done | bytes 2097176
  84.4 39.8 %combine.1 = bf16[4,4,2,128,128]{4,3,2,1,0:T(8,128)(2,1)S(1)} custom-call(f32[4,4,2,128,128]{4,3,2,1,0:T(8,128)S(1)} %bitcast.21, f32[2,32,128]{2,1,0:T(8,128)S(1)} %get-tuple-element.12.ml_ref, bf16[4096,128]{1,0:T(8,128)(2,1)S(1)} %bitcast.19), custom_call_target="tpu_custom_call" | custom-call | tf_op jit(solution)/shard_map/combine/pallas_call | solution.py:363
  124.2 1.2 copy.17
  125.5 0.0 copy-done.1
Async XLA Ops:
  0.6 1.2 copy-start
  3.1 79.7 %all-to-all-start = ((bf16[128,32,128]{2,0,1:T(8,128)(2,1)}), bf16[128,32,128]{2,0,1:T(8,128)(2,1)S(1)}, u32[]{:S(2)}, u32[]{:S(2)}) async-start(bf16[128,32,128]{2,0,1:T(8,128)(2,1)} %copy_bitcast_fusion.1), calls=%async_computation | async-start | bytes 2097152 | tf_op jit(solution)/shard_map/all_to_all | solution.py:338
  12.3 10.5 %copy-start.2 = (bf16[4096,4096]{1,0:T(8,128)(2,1)S(1)}, bf16[4096,4096]{1,0:T(8,128)(2,1)}, u32[]{:S(2)}) copy-start(bf16[4096,4096]{1,0:T(8,128)(2,1)} %wq_hbm.1) | copy-start | bytes 100663296
  22.8 1.2 copy-start.7
  24.0 1.2 copy-start.8
  25.3 1.2 copy-start.9
  26.5 15.3 %copy-start.3 = (bf16[128,256,128]{2,1,0:T(8,128)(2,1)S(1)}, bf16[128,256,128]{2,1,0:T(8,128)(2,1)}, u32[]{:S(2)}) copy-start(bf16[128,256,128]{2,1,0:T(8,128)(2,1)} %k_hbm.1) | copy-start | bytes 25165828
  26.5 15.3 %copy-start.10 = (s32[128]{0:T(128)S(1)}, s32[128]{0:T(128)}, u32[]{:S(2)}) copy-start(s32[128]{0:T(128)} %pos.1) | copy-start | bytes 1540
  41.8 83.7 %copy-start.1 = (bf16[128,4096]{1,0:T(8,128)(2,1)S(1)}, bf16[128,4096]{1,0:T(8,128)(2,1)}, u32[]{:S(2)}) copy-start(bf16[128,4096]{1,0:T(8,128)(2,1)} %param.12) | copy-start | bytes 3145732
  41.8 3.5 %copy-start.4 = (bf16[128,256,128]{2,1,0:T(8,128)(2,1)S(1)}, bf16[128,256,128]{2,1,0:T(8,128)(2,1)}, u32[]{:S(2)}) copy-start(bf16[128,256,128]{2,1,0:T(8,128)(2,1)} %v_hbm.1) | copy-start | bytes 25165828
  81.4 1.3 %copy-start.5 = (f32[4096,128]{1,0:T(8,128)}, f32[4096,128]{1,0:T(8,128)S(1)}, u32[]{:S(2)}) copy-start(f32[4096,128]{1,0:T(8,128)S(1)} %get-tuple-element.11) | copy-start | bytes 6291460
  82.8 1.6 %copy-start.6 = (f32[4096,128]{1,0:T(8,128)S(1)}, f32[4096,128]{1,0:T(8,128)}, u32[]{:S(2)}) copy-start(f32[4096,128]{1,0:T(8,128)} %copy-done.5) | copy-start | bytes 6291460

commit v2 on v1

--- a/solution.py
+++ b/solution.py
@@ -71,9 +71,9 @@
         out = []
         for r in range(1, a):
             if first:
-                srcs = (buf.at[g.y, g.x, g.c, self.lo], buf.at[g.y, g.x, g.c, self.hi])
+                srcs = (buf.at[g.c, g.y, g.x, self.lo], buf.at[g.c, g.y, g.x, self.hi])
             else:
-                srcs = (buf.at[:, g.x, g.c, self.lo], buf.at[g.y, :, g.c, self.hi])
+                srcs = (buf.at[g.c, :, g.x, self.lo], buf.at[g.c, g.y, :, self.hi])
             peers = (g.y_peer(r), g.x_peer(r)) if first else (g.x_peer(r), g.y_peer(r))
             for i in range(2):
                 k = ((0 if first else 2) + i) * (a - 1) + r - 1
@@ -95,7 +95,7 @@
         for cp in second:
             cp.wait_recv()
         k = 4 * (g.a - 1)
-        plane = buf.at[:, :, g.c]
+        plane = buf.at[g.c]
         last = remote(plane, plane, self.send.at[k], self.recv.at[k], g.partner())
         last.start()
         last.wait_recv()
@@ -107,7 +107,7 @@
         return 4 * (a - 1) + 1
 
 
-def project_kernel(n, x_hbm, wq_hbm, wk_hbm, wv_hbm, q_out, kv_out, xv, wqv, wkv, lsem, send, recv):
+def project_kernel(n, x_hbm, wq_hbm, wk_hbm, wv_hbm, wo_hbm, q_out, kv_out, wo_out, xv, wqv, wkv, lsem, wsem, send, recv):
     g = Grid(n)
     hd = wqv.shape[1]
     col = pl.multiple_of(g.me * hd, hd)
@@ -117,25 +117,32 @@
         pltpu.make_async_copy(wk_hbm, wkv.at[:, pl.ds(0, hd)], lsem.at[2]),
         pltpu.make_async_copy(wv_hbm, wkv.at[:, pl.ds(hd, hd)], lsem.at[3]),
     ]
+    rows, width = wo_hbm.shape[0], wo_hbm.shape[1] // 2
+    mine = wo_out.at[pl.ds(pl.multiple_of(g.c * rows, rows), rows)]
+    copies.append(pltpu.make_async_copy(wo_hbm.at[:, pl.ds(pl.multiple_of(g.c * width, width), width)], mine, lsem.at[4]))
     for cp in copies:
         cp.start()
     g.greet()
     copies[0].wait()
     copies[1].wait()
     q = jnp.dot(xv[...], wqv[...], preferred_element_type=F32).astype(BF16)
-    q_out[g.y, g.x, g.c] = q
+    q_out[g.c, g.y, g.x] = q
     g.greeted()
     gather = Gather(g, q_out, send, recv)
     gather.start()
+    swap = remote(wo_hbm.at[:, pl.ds(pl.multiple_of((1 - g.c) * width, width), width)], mine, wsem.at[0], wsem.at[1], g.partner())
+    swap.start()
     copies[2].wait()
     copies[3].wait()
     kv = jnp.dot(xv[...], wkv[...], preferred_element_type=F32).astype(BF16)
     kv_out[0] = kv[:, :hd].astype(F32)
     kv_out[1] = kv[:, hd:].astype(F32)
     gather.finish()
-
-
-def attend_kernel(blk, pos, q_ref, kv_new, k_hbm, v_hbm, ko_hbm, vo_hbm, o_ref, ml_ref, kbuf, vbuf, q32, rsem, wsem):
+    copies[4].wait()
+    swap.wait()
+
+
+def attend_kernel(blk, pos, q_ref, kv_new, k_hbm, v_hbm, ko_hbm, vo_hbm, o_ref, ml_ref, kbuf, vbuf, q32, s_s, w_s, rsem, wsem):
     n_rows, t_loc, hd = kbuf.shape
     n_heads = o_ref.shape[0] // n_rows
     n_blk = n_rows // blk
@@ -164,37 +171,67 @@
     lane_b = lax.broadcasted_iota(jnp.int32, (n_heads, n_rows), 1)
     tile_row = lax.broadcasted_iota(jnp.int32, (16, hd), 0)
 
-    @pl.loop(0, n_blk)
-    def _(i):
+    def intake(i):
         for cp in reads(i):
             cp.wait()
-        slots = []
+        stores = []
         for u in range(blk):
             b = i * blk + u
             p = pos[b] - base
-            slots.append((b, p))
             t0 = pl.multiple_of(jnp.clip(p, 0, t_loc - 1) // 16 * 16, 16)
             hit = tile_row == p - t0
             for which, buf in enumerate((kbuf, vbuf)):
                 new = jnp.broadcast_to(kv_new[which, pl.ds(b, 1), :], (16, hd))
                 old = buf[b, pl.ds(t0, 16), :].astype(F32)
-                buf[b, pl.ds(t0, 16), :] = jnp.where(hit, new, old).astype(BF16)
+                stores.append((buf, b, t0, jnp.where(hit, new, old).astype(BF16)))
+        for buf, b, t0, v in stores:
+            buf[b, pl.ds(t0, 16), :] = v
         for cp in writes(i):
             cp.start()
-        m_acc, l_acc = ml_ref[0], ml_ref[1]
-        for b, p in slots:
-            qb = q32[pl.ds(b, n_heads, stride=n_rows), :].astype(BF16)
-            s = lax.dot_general(qb, kbuf[b], (((1,), (1,)), ((), ())), preferred_element_type=F32) * scale
-            s = jnp.where(lane <= p, s, -jnp.inf)
-            m = jnp.maximum(jnp.max(s, axis=1, keepdims=True), LOWEST)
-            w = jnp.exp2(s - m)
-            l = jnp.sum(w, axis=1, keepdims=True)
-            o = jnp.dot(w.astype(BF16), vbuf[b], preferred_element_type=F32)
+
+    def step(i, qk, soft, pv):
+        outs, scores = [], []
+        if pv:
+            for u in range(blk):
+                b = (i - 2) * blk + u
+                outs.append((b, jnp.dot(w_s[u], vbuf[b], preferred_element_type=F32)))
+        if soft:
+            m_acc, l_acc = ml_ref[0], ml_ref[1]
+            ss = [s_s[u] for u in range(blk)]
+        if qk:
+            for u in range(blk):
+                b = i * blk + u
+                qb = q32[pl.ds(b, n_heads, stride=n_rows), :].astype(BF16)
+                scores.append(lax.dot_general(qb, kbuf[b], (((1,), (1,)), ((), ())), preferred_element_type=F32))
+        if soft:
+            for u, s in enumerate(ss):
+                b = (i - 1) * blk + u
+                s = jnp.where(lane <= pos[b] - base, s * scale, -jnp.inf)
+                m = jnp.maximum(jnp.max(s, axis=1, keepdims=True), LOWEST)
+                w = jnp.exp2(s - m)
+                l = jnp.sum(w, axis=1, keepdims=True)
+                w_s[u] = w.astype(BF16)
+                m_acc = jnp.where(lane_b == b, m, m_acc)
+                l_acc = jnp.where(lane_b == b, l, l_acc)
+            ml_ref[0] = m_acc
+            ml_ref[1] = l_acc
+        for u, s in enumerate(scores):
+            s_s[u] = s
+        for b, o in outs:
             o_ref[pl.ds(b, n_heads, stride=n_rows), :] = o
-            m_acc = jnp.where(lane_b == b, m, m_acc)
-            l_acc = jnp.where(lane_b == b, l, l_acc)
-        ml_ref[0] = m_acc
-        ml_ref[1] = l_acc
+
+    intake(0)
+    step(0, True, False, False)
+    intake(1)
+    step(1, True, True, False)
+
+    @pl.loop(2, n_blk)
+    def _(i):
+        intake(i)
+        step(i, True, True, True)
+
+    step(n_blk, False, True, True)
+    step(n_blk + 1, False, False, True)
 
     @pl.loop(0, n_blk)
     def _(i):
@@ -209,7 +246,7 @@
     return top, fs, total
 
 
-def combine_kernel(n, o_ref, ml_ref, wo_ref, y_out, r0, ml0, rows, fa, fb, fcol, mla, mlb, r1a, r1b, rmla, rmlb, s2a, s2b, sm2a, sm2b, r2a, r2b, rm2a, rm2b, go, send0, recv0, send1, recv1, send2, recv2, asend, arecv, bsend, brecv):
+def combine_kernel(n, o_ref, ml_ref, wo_ref, y_out, r0, ml0, rows, fa, fb, fcol, mla, mlb, r1a, r1b, rmla, rmlb, s2a, s2b, sm2a, sm2b, r2a, r2b, rm2a, rm2b, go, r0y, y1a, y1b, t2a, t2b, y2a, y2b, send0, recv0, send1, recv1, send2, recv2, osem, send3, recv3, send4, recv4, bsend, brecv):
     g = Grid(n)
     a = g.a
     n_rows, hd = o_ref.shape[3:]
@@ -224,12 +261,12 @@
     core_a, core_b = {}, {}
     for r in order:
         hy, hx = g.y_at(r + 1), g.x_at(r + 1)
-        core_a[r] = remote(o_ref.at[hy, :, 1 - g.c, lo], r0.at[hy, :, lo], send0.at[r], recv0.at[r], g.partner())
-        core_b[r] = remote(o_ref.at[:, hx, 1 - g.c, hi], r0.at[:, hx, hi], send0.at[a + r], recv0.at[a + r], g.partner())
+        core_a[r] = remote(o_ref.at[1 - g.c, hy, :, lo], r0.at[hy, :, lo], send0.at[r], recv0.at[r], g.partner())
+        core_b[r] = remote(o_ref.at[1 - g.c, :, hx, hi], r0.at[:, hx, hi], send0.at[a + r], recv0.at[a + r], g.partner())
         core_a[r].start()
         core_b[r].start()
     ml_cp.wait_recv()
-    own = pl.ds(g.c, a * a, stride=2)
+    own = pl.ds(pl.multiple_of(g.c * a * a, a * a), a * a)
     top, fs, total = merge([ml_ref[0, own, :], ml0[0, own, :]], [ml_ref[1, own, :], ml0[1, own, :]])
     for i, v in enumerate([top, total] + fs):
         rows[i] = v
@@ -245,7 +282,7 @@
         core_a[r].wait_recv()
         ft = fa[hy].T[:half]
         for j in range(a):
-            r0[hy, j, lo] = o_ref[hy, j, g.c, lo] * ft[:, j:j + 1] + r0[hy, j, lo] * ft[:, a + j:a + j + 1]
+            r0[hy, j, lo] = o_ref[g.c, hy, j, lo] * ft[:, j:j + 1] + r0[hy, j, lo] * ft[:, a + j:a + j + 1]
         if r < a - 1:
             ring1 += [
                 remote(mla.at[hy], rmla.at[r], send1.at[0, r], recv1.at[0, r], g.y_peer(r + 1)),
@@ -256,7 +293,7 @@
         core_b[r].wait_recv()
         ft = fb[hx].T[half:]
         for j in range(a):
-            r0[j, hx, hi] = o_ref[j, hx, g.c, hi] * ft[:, j:j + 1] + r0[j, hx, hi] * ft[:, a + j:a + j + 1]
+            r0[j, hx, hi] = o_ref[g.c, j, hx, hi] * ft[:, j:j + 1] + r0[j, hx, hi] * ft[:, a + j:a + j + 1]
         if r < a - 1:
             ring1 += [
                 remote(mlb.at[hx], rmlb.at[r], send1.at[2, r], recv1.at[2, r], g.x_peer(r + 1)),
@@ -309,20 +346,45 @@
         acc = mine[place] * ft[:, 0:1]
         for r in range(a - 1):
             acc = acc + got[r] * ft[:, r + 1:r + 2]
-        go[g.y, g.x, g.c, (hi if side else lo), :] = (acc / ft[:, a:a + 1]).astype(BF16)
-
-    heads = Gather(g, go, asend, arecv)
+        go[g.c, (hi if side else lo), :] = (acc / ft[:, a:a + 1]).astype(BF16)
+
+    heads = remote(go.at[g.c], go.at[g.c], osem.at[0], osem.at[1], g.partner())
     heads.start()
-    heads.finish()
-    acc = jnp.zeros((n_rows, wo_ref.shape[1]), F32)
-    for k in range(a * a):
-        lhs = jnp.concatenate([go[k // a, k % a, 0], go[k // a, k % a, 1]], axis=1)
-        acc = acc + jnp.dot(lhs, wo_ref[pl.ds(k * 2 * hd, 2 * hd), :], preferred_element_type=F32)
-    y_out[g.y, g.x, g.c] = acc.astype(BF16)
+    heads.wait_recv()
+    lhs = jnp.concatenate([go[0], go[1]], axis=1)
+    for i in range(a):
+        part = jnp.dot(lhs, wo_ref[:, pl.ds(i * a * hd, a * hd)], preferred_element_type=F32)
+        for j in range(a):
+            r0y[i, j] = part[:, j * hd:(j + 1) * hd]
+    ring3, ring4 = [], []
+    for r in order[:-1]:
+        hy, hx = g.y_at(r + 1), g.x_at(r + 1)
+        ring3 += [
+            remote(r0y.at[hy, :, lo], y1a.at[r], send3.at[0, r], recv3.at[0, r], g.y_peer(r + 1)),
+            remote(r0y.at[:, hx, hi], y1b.at[r], send3.at[1, r], recv3.at[1, r], g.x_peer(r + 1)),
+        ]
+    for cp in ring3:
+        cp.start()
+    for cp in ring3:
+        cp.wait_recv()
+    t2a[...] = functools.reduce(jnp.add, [y1a[r] for r in range(a - 1)], r0y[g.y, :, lo])
+    t2b[...] = functools.reduce(jnp.add, [y1b[r] for r in range(a - 1)], r0y[:, g.x, hi])
+    for r in order[:-1]:
+        hy, hx = g.y_at(r + 1), g.x_at(r + 1)
+        ring4 += [
+            remote(t2a.at[hx], y2a.at[r], send4.at[0, r], recv4.at[0, r], g.x_peer(r + 1)),
+            remote(t2b.at[hy], y2b.at[r], send4.at[1, r], recv4.at[1, r], g.y_peer(r + 1)),
+        ]
+    for cp in ring4:
+        cp.start()
+    for cp in ring4:
+        cp.wait_recv()
+    y_out[g.c, g.y, g.x, lo, :] = functools.reduce(jnp.add, [y2a[r] for r in range(a - 1)], t2a[g.x]).astype(BF16)
+    y_out[g.c, g.y, g.x, hi, :] = functools.reduce(jnp.add, [y2b[r] for r in range(a - 1)], t2b[g.y]).astype(BF16)
     outs = Gather(g, y_out, bsend, brecv)
     outs.start()
     outs.finish()
-    for cp in [ml_cp] + list(core_a.values()) + list(core_b.values()) + ring1 + ring2:
+    for cp in [ml_cp, heads] + list(core_a.values()) + list(core_b.values()) + ring1 + ring2 + ring3 + ring4:
         cp.wait_send()
 
 
@@ -332,48 +394,51 @@
     vmem, hbm, smem = (pl.BlockSpec(memory_space=s) for s in (pltpu.VMEM, pltpu.HBM, pltpu.SMEM))
     dma = pltpu.SemaphoreType.DMA
 
+    def stay(x):
+        return pltpu.with_memory_space_constraint(x, pltpu.HBM)
+
     def local_step(tokens, w_query, w_key, w_value, w_out, k_cache, v_cache, positions):
         n_rows, t_loc, hd = k_cache.shape
         d_model = tokens.shape[1]
-        wo = lax.all_to_all(w_out.reshape(w_out.shape[0], n, -1), 'sp', split_axis=1, concat_axis=0, tiled=True)
-        wo = wo.reshape(w_out.shape[0] * n, -1)
         half = n_rows // 2
+        f32 = lambda *s: pltpu.VMEM(s, F32)
+        bf16 = lambda *s: pltpu.VMEM(s, BF16)
+        shape = jax.ShapeDtypeStruct
         sems = [dma((Gather.sems(a),))] * 2
-        q_all, kv_new = pl.pallas_call(
+        q_all, kv_new, wo = pl.pallas_call(
             functools.partial(project_kernel, n),
-            out_shape=(jax.ShapeDtypeStruct((a, a, 2, n_rows, hd), BF16), jax.ShapeDtypeStruct((2, n_rows, hd), F32)),
-            in_specs=[hbm] * 4,
-            out_specs=(vmem, vmem),
-            scratch_shapes=[pltpu.VMEM((n_rows, d_model), BF16), pltpu.VMEM((d_model, hd), BF16), pltpu.VMEM((d_model, 2 * hd), BF16), dma((4,))] + sems,
-            compiler_params=pltpu.CompilerParams(collective_id=0, has_side_effects=True, vmem_limit_bytes=10 << 20),
+            out_shape=(shape((2, a, a, n_rows, hd), BF16), shape((2, n_rows, hd), F32), shape((2 * w_out.shape[0], w_out.shape[1] // 2), BF16)),
+            in_specs=[hbm] * 5,
+            out_specs=(vmem,) * 3,
+            scratch_shapes=[bf16(n_rows, d_model), bf16(d_model, hd), bf16(d_model, 2 * hd), dma((5,)), dma((2,))] + sems,
+            compiler_params=pltpu.CompilerParams(collective_id=0, has_side_effects=True, vmem_limit_bytes=12 << 20),
             name='project',
-        )(tokens, w_query, w_key, w_value)
+        )(*map(stay, (tokens, w_query, w_key, w_value, w_out)))
         blk = 8
-        cache = jax.ShapeDtypeStruct(k_cache.shape, k_cache.dtype)
+        cache = shape(k_cache.shape, k_cache.dtype)
         k_upd, v_upd, o, ml = pl.pallas_call(
             functools.partial(attend_kernel, blk),
-            out_shape=(cache, cache, jax.ShapeDtypeStruct((n * n_rows, hd), F32), jax.ShapeDtypeStruct((2, n, n_rows), F32)),
+            out_shape=(cache, cache, shape((n * n_rows, hd), F32), shape((2, n, n_rows), F32)),
             in_specs=[smem, vmem, vmem, hbm, hbm],
             out_specs=(hbm, hbm, vmem, vmem),
-            scratch_shapes=[pltpu.VMEM(k_cache.shape, BF16)] * 2 + [pltpu.VMEM((n * n_rows, hd), F32)] + [dma((2, n_rows // blk))] * 2,
+            scratch_shapes=[bf16(*k_cache.shape)] * 2 + [f32(n * n_rows, hd), f32(blk, n, t_loc), bf16(blk, n, t_loc)] + [dma((2, n_rows // blk))] * 2,
             compiler_params=pltpu.CompilerParams(vmem_limit_bytes=28 << 20),
             name='attend',
-        )(positions, q_all.reshape(n, n_rows, hd), kv_new, k_cache, v_cache)
-        f32 = lambda *s: pltpu.VMEM(s, F32)
+        )(positions, q_all.reshape(n, n_rows, hd), kv_new, stay(k_cache), stay(v_cache))
         y = pl.pallas_call(
             functools.partial(combine_kernel, n),
-            out_shape=jax.ShapeDtypeStruct((a, a, 2, n_rows, w_out.shape[1] // n), BF16),
+            out_shape=shape((2, a, a, n_rows, w_out.shape[1] // n), BF16),
             in_specs=[vmem] * 3,
             out_specs=vmem,
             scratch_shapes=[f32(a, a, n_rows, hd), f32(2, n, n_rows), f32(4, a * a, n_rows)]
             + [f32(a, 2 * a, n_rows)] * 2 + [f32(max(a * a, 8), n_rows)] + [f32(a, 2 * a, n_rows)] * 2
             + [f32(a - 1, a, half, hd)] * 2 + [f32(a - 1, 2 * a, n_rows)] * 2
             + [f32(a, half, hd)] * 2 + [f32(a, 8, n_rows)] * 2 + [f32(a - 1, half, hd)] * 2 + [f32(a - 1, 8, n_rows)] * 2
-            + [pltpu.VMEM((a, a, 2, n_rows, hd), BF16)]
-            + [dma((2 * a + 1,))] * 2 + [dma((4, a - 1))] * 4 + sems * 2,
-            compiler_params=pltpu.CompilerParams(collective_id=1, has_side_effects=True, vmem_limit_bytes=14 << 20),
+            + [bf16(2, n_rows, hd), f32(a, a, n_rows, hd)] + [f32(a - 1, a, half, hd)] * 2 + [f32(a, half, hd)] * 2 + [f32(a - 1, half, hd)] * 2
+            + [dma((2 * a + 1,))] * 2 + [dma((4, a - 1))] * 4 + [dma((2,))] + [dma((2, a - 1))] * 4 + sems,
+            compiler_params=pltpu.CompilerParams(collective_id=1, has_side_effects=True, vmem_limit_bytes=16 << 20),
             name='combine',
-        )(o.reshape(a, a, 2, n_rows, hd), ml, wo)
+        )(o.reshape(2, a, a, n_rows, hd), ml, wo)
         y = y.reshape(n, n_rows, -1).transpose(1, 0, 2).reshape(n_rows, -1)
         return y, k_upd, v_upd
 

time: 126 us -> 75.2 us (0.60)
  local copies, waits for them, and re-layouts: 24.3 us -> 1.25 us
  Pallas kernels: 91.3 us -> 73.2 us
  starting transfers between devices: 9.14 us -> 0 us
    pallas_call x1, Pallas kernels: 36.1 us -> 13 us  [local_step(): pl.pallas_call(functools.partial(attend_kernel, blk), out_shape=(cache, c...]
    unnamed x22 -> x2, local copies, waits for them, and re-layouts: 21.8 us -> 0.01 us
    all_to_all x1 -> x0, starting transfers between devices: 9.14 us -> none  [local_step(): lax.all_to_all(w_out.reshape(w_out.shape[0], n, -1), 'sp', split_axis=1,...]
    pallas_call x2, Pallas kernels: 55.1 us -> 60.2 us  [the longest x1 42.1 us: local_step(): pl.pallas_call(functools.partial(combine_kernel, n), out_shape=shape((2,...]
    reshape x1 -> x0, local copies, waits for them, and re-layouts: 1.26 us -> none  [local_step(): w_out.reshape(w_out.shape[0], n, -1)]
  transfers between devices with their start and end apart: 1 -> 0, of which waited for: 0 -> 0; matrix products, arithmetic and copies ran while one was open for 0% -> 0% of each run, Pallas kernels for 41% -> 0%
where the time goes in v2:
time: 75.2 us; the launch traced here: 75.1 us
  Pallas kernels  73.2 us (97%)
  local copies, waits for them, and re-layouts  1.25 us (2%)
    pallas_call x1, Pallas kernels, local_step(): pl.pallas_call(functools.partial(combine_kernel, n), out_shape=shape((2,...  42.1 us
    pallas_call x1, Pallas kernels, local_step(): pl.pallas_call(functools.partial(project_kernel, n), out_shape=(shape((2,...  18.2 us
    pallas_call x1, Pallas kernels, local_step(): pl.pallas_call(functools.partial(attend_kernel, blk), out_shape=(cache, c...  13 us

profile of v2, /device:TPU:97, one launch (start us, length us, event | category | flops | bytes accessed | tf_op | source)
XLA Modules:
  0.0 75.1 jit_solution(213479635664631650)
XLA Ops:
  0.6 0.0 copy-start
  0.6 18.2 %project.1 = (bf16[2,4,4,128,128]{4,3,2,1,0:T(8,128)(2,1)S(1)}, f32[2,128,128]{2,1,0:T(8,128)S(1)}, bf16[256,2048]{1,0:T(8,128)(2,1)S(1)}) custom-call(bf16[128,4096]{1,0:T(8,128)(2,1)} %x_hbm.1, bf16[4096,4096]{1,0:T(8,128)(2,1)} %wq_hbm.1, bf16[4096,128]{1,0:T(8,128)(2,1)} %wk_hbm.1, bf16[4096,128]{1,0:T(8,128)(2,1)} %wv_hbm.1, bf16[128,4096]{1,0:T(8,128)(2,1)} %wo_hbm.1), custom_call_target="tpu_custom_call" | custom-call | tf_op jit(solution)/shard_map/project/pallas_call | solution.py:408
  18.8 0.0 copy-done
  18.8 13.0 %attend.1 = (bf16[128,256,128]{2,1,0:T(8,128)(2,1)}, bf16[128,256,128]{2,1,0:T(8,128)(2,1)}, f32[4096,128]{1,0:T(8,128)S(1)}, f32[2,32,128]{2,1,0:T(8,128)S(1)}) custom-call(s32[128]{0:T(128)S(1)} %copy-done, bf16[32,128,128]{2,1,0:T(8,128)(2,1)S(1)} %bitcast.11, f32[2,128,128]{2,1,0:T(8,128)S(1)} %get-tuple-element.11.kv_new, bf16[128,256,128]{2,1,0:T(8,128)(2,1)} %k_hbm.1, ...), custom_call_target="tpu_custom_call" | custom-call | tf_op jit(solution)/shard_map/attend/pallas_call | solution.py:419
  31.8 42.1 %combine.1 = bf16[2,4,4,128,128]{4,3,2,1,0:T(8,128)(2,1)S(1)} custom-call(f32[2,4,4,128,128]{4,3,2,1,0:T(8,128)S(1)} %bitcast.10, f32[2,32,128]{2,1,0:T(8,128)S(1)} %get-tuple-element.13.ml_ref, bf16[256,2048]{1,0:T(8,128)(2,1)S(1)} %get-tuple-element.14.wo_ref), custom_call_target="tpu_custom_call" | custom-call | tf_op jit(solution)/shard_map/combine/pallas_call | solution.py:428
  73.9 1.2 %copy.14 = bf16[32,16,8,128]{3,2,0,1:T(8,128)(2,1)} copy(bf16[32,16,8,128]{3,2,1,0:T(8,128)(2,1)S(1)} %bitcast.9) | data formatting | bytes 2097152 | tf_op jit(solution)/shard_map/reshape | solution.py:442
Async XLA Ops:
  0.6 18.2 %copy-start = (s32[128]{0:T(128)S(1)}, s32[128]{0:T(128)}, u32[]{:S(2)}) copy-start(s32[128]{0:T(128)} %pos.1) | copy-start | bytes 1540

commit v3 on v2

--- a/solution.py
+++ b/solution.py
@@ -64,103 +64,115 @@
     def __init__(self, g, buf, send, recv):
         self.g, self.buf, self.send, self.recv = g, buf, send, recv
         rows = buf.shape[3]
-        self.lo, self.hi = pl.ds(0, rows // 2), pl.ds(rows // 2, rows // 2)
-
-    def ring_copies(self, first):
+        self.half = (pl.ds(0, rows // 2), pl.ds(rows // 2, rows // 2))
+        self.order = sorted(range(1, g.a), key=lambda r: -min(r, g.a - r))
+        self.k = 0
+
+    def cp(self, ref, dev):
+        c = remote(ref, ref, self.send.at[self.k], self.recv.at[self.k], dev)
+        self.k += 1
+        c.start()
+        return c
+
+    def start(self):
+        g, buf = self.g, self.buf
+        self.first, self.late = {}, []
+        for r in self.order:
+            self.first[0, r] = self.cp(buf.at[g.c, g.y, g.x, self.half[0]], g.y_peer(r))
+            self.first[1, r] = self.cp(buf.at[g.c, g.y, g.x, self.half[1]], g.x_peer(r))
+        for r in self.order:
+            self.late.append(((0, 0, r), self.cp(buf.at[g.c, g.y, g.x, self.half[0]], g.x_peer(r))))
+            self.late.append(((1, 0, r), self.cp(buf.at[g.c, g.y, g.x, self.half[1]], g.y_peer(r))))
+        self.core = [self.cp(buf.at[g.c, g.y, g.x], g.partner())]
+
+    def finish(self):
         g, buf, a = self.g, self.buf, self.g.a
-        out = []
-        for r in range(1, a):
-            if first:
-                srcs = (buf.at[g.c, g.y, g.x, self.lo], buf.at[g.c, g.y, g.x, self.hi])
+        for r in self.order[::-1]:
+            for s in range(2):
+                self.first[s, r].wait_recv()
+                src = buf.at[g.c, g.y_at(a - r), g.x, self.half[0]] if s == 0 else buf.at[g.c, g.y, g.x_at(a - r), self.half[1]]
+                for q in self.order:
+                    self.late.append(((s, r, q), self.cp(src, g.x_peer(q) if s == 0 else g.y_peer(q))))
+                self.core.append(self.cp(src, g.partner()))
+        for (s, r, q), c in self.late:
+            c.wait_recv()
+            if s == 0:
+                src = buf.at[g.c, g.y_at((a - r) % a), g.x_at(a - q), self.half[0]]
             else:
-                srcs = (buf.at[g.c, :, g.x, self.lo], buf.at[g.c, g.y, :, self.hi])
-            peers = (g.y_peer(r), g.x_peer(r)) if first else (g.x_peer(r), g.y_peer(r))
-            for i in range(2):
-                k = ((0 if first else 2) + i) * (a - 1) + r - 1
-                out.append(remote(srcs[i], srcs[i], self.send.at[k], self.recv.at[k], peers[i]))
-        return out
-
-    def start(self):
-        self.first = self.ring_copies(True)
-        for cp in self.first:
-            cp.start()
-
-    def finish(self):
-        g, buf = self.g, self.buf
-        for cp in self.first:
-            cp.wait_recv()
-        second = self.ring_copies(False)
-        for cp in second:
-            cp.start()
-        for cp in second:
-            cp.wait_recv()
-        k = 4 * (g.a - 1)
-        plane = buf.at[g.c]
-        last = remote(plane, plane, self.send.at[k], self.recv.at[k], g.partner())
-        last.start()
-        last.wait_recv()
-        for cp in self.first + second + [last]:
-            cp.wait_send()
+                src = buf.at[g.c, g.y_at(a - q), g.x_at((a - r) % a), self.half[1]]
+            self.core.append(self.cp(src, g.partner()))
+        for c in self.core:
+            c.wait_recv()
+        for c in list(self.first.values()) + [c for _, c in self.late] + self.core:
+            c.wait_send()
 
     @staticmethod
     def sems(a):
-        return 4 * (a - 1) + 1
-
-
-def project_kernel(n, x_hbm, wq_hbm, wk_hbm, wv_hbm, wo_hbm, q_out, kv_out, wo_out, xv, wqv, wkv, lsem, wsem, send, recv):
+        return 4 * (a - 1) + 1 + 2 * (a - 1) * a + 2 * (a - 1) * a
+
+
+def project_kernel(n, x_hbm, wq_hbm, wk_hbm, wv_hbm, wo_hbm, k_hbm, v_hbm, q_out, kv_out, wo_out, k_out, v_out, xv, wqv, wkv, lsem, qsem, csem, rsem):
     g = Grid(n)
-    hd = wqv.shape[1]
-    col = pl.multiple_of(g.me * hd, hd)
-    copies = [
-        pltpu.make_async_copy(x_hbm, xv, lsem.at[0]),
-        pltpu.make_async_copy(wq_hbm.at[:, pl.ds(col, hd)], wqv, lsem.at[1]),
-        pltpu.make_async_copy(wk_hbm, wkv.at[:, pl.ds(0, hd)], lsem.at[2]),
-        pltpu.make_async_copy(wv_hbm, wkv.at[:, pl.ds(hd, hd)], lsem.at[3]),
+    hd = kv_out.shape[2]
+    width = wq_hbm.shape[1] // 2
+    n_part, part = wqv.shape[0], wqv.shape[2]
+    x_cp = pltpu.make_async_copy(x_hbm, xv, lsem.at[0])
+    q_cps = [
+        pltpu.make_async_copy(wq_hbm.at[:, pl.ds(pl.multiple_of(g.c * width + i * part, part), part)], wqv.at[i], qsem.at[i])
+        for i in range(n_part)
     ]
-    rows, width = wo_hbm.shape[0], wo_hbm.shape[1] // 2
+    kv_cps = [
+        pltpu.make_async_copy(wk_hbm, wkv.at[:, pl.ds(0, hd)], lsem.at[1]),
+        pltpu.make_async_copy(wv_hbm, wkv.at[:, pl.ds(hd, hd)], lsem.at[2]),
+    ]
+    rows, half = wo_hbm.shape[0], wo_hbm.shape[1] // 2
     mine = wo_out.at[pl.ds(pl.multiple_of(g.c * rows, rows), rows)]
-    copies.append(pltpu.make_async_copy(wo_hbm.at[:, pl.ds(pl.multiple_of(g.c * width, width), width)], mine, lsem.at[4]))
-    for cp in copies:
+    wo_cp = pltpu.make_async_copy(wo_hbm.at[:, pl.ds(pl.multiple_of(g.c * half, half), half)], mine, lsem.at[3])
+    wo_swap = remote(wo_hbm.at[:, pl.ds(pl.multiple_of((1 - g.c) * half, half), half)], mine, rsem.at[0], rsem.at[1], g.partner())
+    cache_cps = [pltpu.make_async_copy(k_hbm, k_out, csem.at[0]), pltpu.make_async_copy(v_hbm, v_out, csem.at[1])]
+    x_cp.start()
+    for cp in q_cps + kv_cps:
         cp.start()
-    g.greet()
-    copies[0].wait()
-    copies[1].wait()
-    q = jnp.dot(xv[...], wqv[...], preferred_element_type=F32).astype(BF16)
-    q_out[g.c, g.y, g.x] = q
-    g.greeted()
-    gather = Gather(g, q_out, send, recv)
-    gather.start()
-    swap = remote(wo_hbm.at[:, pl.ds(pl.multiple_of((1 - g.c) * width, width), width)], mine, wsem.at[0], wsem.at[1], g.partner())
-    swap.start()
-    copies[2].wait()
-    copies[3].wait()
+    barrier = pltpu.get_barrier_semaphore()
+    pl.semaphore_signal(barrier, inc=1, device_id={'sp': g.partner()}, device_id_type=MESH)
+    x_cp.wait()
+    per = part // hd
+    first = g.c * (n // 4)
+    for i in range(n_part):
+        q_cps[i].wait()
+        if i == n_part - 2:
+            cache_cps[0].start()
+        q = jnp.dot(xv[...], wqv[i], preferred_element_type=F32).astype(BF16)
+        for j in range(i * per, (i + 1) * per):
+            q_out[j % 2, first + j // 2] = q[:, (j - i * per) * hd:(j - i * per + 1) * hd]
+    cache_cps[1].start()
+    pl.semaphore_wait(barrier, 1)
+    heads = q_out.at[:, pl.ds(first, n // 4)]
+    q_swap = remote(heads, heads, rsem.at[2], rsem.at[3], g.partner())
+    q_swap.start()
+    wo_swap.start()
+    wo_cp.start()
+    for cp in kv_cps:
+        cp.wait()
     kv = jnp.dot(xv[...], wkv[...], preferred_element_type=F32).astype(BF16)
     kv_out[0] = kv[:, :hd].astype(F32)
     kv_out[1] = kv[:, hd:].astype(F32)
-    gather.finish()
-    copies[4].wait()
-    swap.wait()
-
-
-def attend_kernel(blk, pos, q_ref, kv_new, k_hbm, v_hbm, ko_hbm, vo_hbm, o_ref, ml_ref, kbuf, vbuf, q32, s_s, w_s, rsem, wsem):
+    q_swap.wait()
+    wo_swap.wait()
+    for cp in [wo_cp] + cache_cps:
+        cp.wait()
+
+
+def attend_kernel(blk, pos, q_ref, kv_new, k_in, v_in, ko_hbm, vo_hbm, o_ref, ml_ref, kbuf, vbuf, q32, s_s, w_s, wsem):
     n_rows, t_loc, hd = kbuf.shape
     n_heads = o_ref.shape[0] // n_rows
     n_blk = n_rows // blk
     base = lax.axis_index('sp') * t_loc
     scale = hd ** -0.5 * math.log2(math.e)
 
-    def reads(i):
-        rows = pl.ds(i * blk, blk)
-        return (pltpu.make_async_copy(k_hbm.at[rows], kbuf.at[rows], rsem.at[0, i]), pltpu.make_async_copy(v_hbm.at[rows], vbuf.at[rows], rsem.at[1, i]))
-
     def writes(i):
         rows = pl.ds(i * blk, blk)
         return (pltpu.make_async_copy(kbuf.at[rows], ko_hbm.at[rows], wsem.at[0, i]), pltpu.make_async_copy(vbuf.at[rows], vo_hbm.at[rows], wsem.at[1, i]))
-
-    @pl.loop(0, n_blk)
-    def _(i):
-        for cp in reads(i):
-            cp.start()
 
     @pl.loop(0, n_heads)
     def _(h):
@@ -172,8 +184,6 @@
     tile_row = lax.broadcasted_iota(jnp.int32, (16, hd), 0)
 
     def intake(i):
-        for cp in reads(i):
-            cp.wait()
         stores = []
         for u in range(blk):
             b = i * blk + u
@@ -404,27 +414,29 @@
         f32 = lambda *s: pltpu.VMEM(s, F32)
         bf16 = lambda *s: pltpu.VMEM(s, BF16)
         shape = jax.ShapeDtypeStruct
+        blk = 16
         sems = [dma((Gather.sems(a),))] * 2
-        q_all, kv_new, wo = pl.pallas_call(
+        cache = shape(k_cache.shape, k_cache.dtype)
+        n_part = 4
+        q_all, kv_new, wo, k_vm, v_vm = pl.pallas_call(
             functools.partial(project_kernel, n),
-            out_shape=(shape((2, a, a, n_rows, hd), BF16), shape((2, n_rows, hd), F32), shape((2 * w_out.shape[0], w_out.shape[1] // 2), BF16)),
-            in_specs=[hbm] * 5,
-            out_specs=(vmem,) * 3,
-            scratch_shapes=[bf16(n_rows, d_model), bf16(d_model, hd), bf16(d_model, 2 * hd), dma((5,)), dma((2,))] + sems,
-            compiler_params=pltpu.CompilerParams(collective_id=0, has_side_effects=True, vmem_limit_bytes=12 << 20),
+            out_shape=(shape((2, n // 2, n_rows, hd), BF16), shape((2, n_rows, hd), F32), shape((2 * w_out.shape[0], w_out.shape[1] // 2), BF16), cache, cache),
+            in_specs=[hbm] * 7,
+            out_specs=(vmem,) * 5,
+            scratch_shapes=[bf16(n_rows, d_model), bf16(n_part, d_model, w_query.shape[1] // 2 // n_part), bf16(d_model, 2 * hd), dma((4,)), dma((n_part,)), dma((2,)), dma((4,))],
+            compiler_params=pltpu.CompilerParams(collective_id=0, has_side_effects=True, vmem_limit_bytes=22 << 20),
             name='project',
-        )(*map(stay, (tokens, w_query, w_key, w_value, w_out)))
-        blk = 8
-        cache = shape(k_cache.shape, k_cache.dtype)
-        k_upd, v_upd, o, ml = pl.pallas_call(
+        )(*map(stay, (tokens, w_query, w_key, w_value, w_out, k_cache, v_cache)))
+        k_upd, v_upd, o, ml, _, _ = pl.pallas_call(
             functools.partial(attend_kernel, blk),
-            out_shape=(cache, cache, shape((n * n_rows, hd), F32), shape((2, n, n_rows), F32)),
-            in_specs=[smem, vmem, vmem, hbm, hbm],
-            out_specs=(hbm, hbm, vmem, vmem),
-            scratch_shapes=[bf16(*k_cache.shape)] * 2 + [f32(n * n_rows, hd), f32(blk, n, t_loc), bf16(blk, n, t_loc)] + [dma((2, n_rows // blk))] * 2,
-            compiler_params=pltpu.CompilerParams(vmem_limit_bytes=28 << 20),
+            out_shape=(cache, cache, shape((n * n_rows, hd), F32), shape((2, n, n_rows), F32), cache, cache),
+            in_specs=[smem] + [vmem] * 4,
+            out_specs=(hbm, hbm) + (vmem,) * 4,
+            input_output_aliases={3: 4, 4: 5},
+            scratch_shapes=[f32(n * n_rows, hd), f32(blk, n, t_loc), bf16(blk, n, t_loc)] + [dma((2, n_rows // blk))],
+            compiler_params=pltpu.CompilerParams(vmem_limit_bytes=8 << 20),
             name='attend',
-        )(positions, q_all.reshape(n, n_rows, hd), kv_new, stay(k_cache), stay(v_cache))
+        )(positions, q_all.reshape(n, n_rows, hd), kv_new, k_vm, v_vm)
         y = pl.pallas_call(
             functools.partial(combine_kernel, n),
             out_shape=shape((2, a, a, n_rows, w_out.shape[1] // n), BF16),

time: 75.2 us -> 69.2 us (0.920)
  Pallas kernels: 73.2 us -> 67.2 us
    pallas_call x1, Pallas kernels: 18.2 us -> 12 us  [local_step(): pl.pallas_call(functools.partial(project_kernel, n), out_shape=(shape((2,...]
    pallas_call x1, Pallas kernels: 42.1 us -> 46.9 us  [local_step(): pl.pallas_call(functools.partial(combine_kernel, n), out_shape=shape((2,...]
    pallas_call x1, Pallas kernels: 13 us -> 8.27 us  [local_step(): pl.pallas_call(functools.partial(attend_kernel, blk), out_shape=(cache, c...]
where the time goes in v3:
time: 69.2 us; the launch traced here: 69.1 us
  Pallas kernels  67.2 us (97%)
  local copies, waits for them, and re-layouts  1.25 us (2%)
    pallas_call x1, Pallas kernels, local_step(): pl.pallas_call(functools.partial(combine_kernel, n), out_shape=shape((2,...  46.9 us
    pallas_call x1, Pallas kernels, local_step(): pl.pallas_call(functools.partial(project_kernel, n), out_shape=(shape((2,...  12 us
    pallas_call x1, Pallas kernels, local_step(): pl.pallas_call(functools.partial(attend_kernel, blk), out_shape=(cache, c...  8.27 us

profile of v3, /device:TPU:97, one launch (start us, length us, event | category | flops | bytes accessed | tf_op | source)
XLA Modules:
  0.0 69.1 jit_solution(5156651970180144528)
XLA Ops:
  0.6 0.0 copy-start
  0.6 12.0 %project.1 = (bf16[2,16,128,128]{3,2,1,0:T(8,128)(2,1)S(1)}, f32[2,128,128]{2,1,0:T(8,128)S(1)}, bf16[256,2048]{1,0:T(8,128)(2,1)S(1)}, bf16[128,256,128]{2,1,0:T(8,128)(2,1)S(1)}, bf16[128,256,128]{2,1,0:T(8,128)(2,1)S(1)}) custom-call(bf16[128,4096]{1,0:T(8,128)(2,1)} %x_hbm.1, bf16[4096,4096]{1,0:T(8,128)(2,1)} %wq_hbm.1, bf16[4096,128]{1,0:T(8,128)(2,1)} %wk_hbm.1, ...), custom_call_target="tpu_custom_call" | custom-call | tf_op jit(solution)/shard_map/project/pallas_call | solution.py:421
  12.7 0.0 copy-done
  12.7 8.3 %attend.1 = (bf16[128,256,128]{2,1,0:T(8,128)(2,1)}, bf16[128,256,128]{2,1,0:T(8,128)(2,1)}, f32[4096,128]{1,0:T(8,128)S(1)}, f32[2,32,128]{2,1,0:T(8,128)S(1)},...) custom-call(s32[128]{0:T(128)S(1)} %copy-done, ...), custom_call_target="tpu_custom_call", output_to_operand_aliasing={{4}: (3, {}), {5}: (4, {})} | custom-call | tf_op jit(solution)/shard_map/attend/pallas_call | solution.py:430
  20.9 46.9 %combine.1 = bf16[2,4,4,128,128]{4,3,2,1,0:T(8,128)(2,1)S(1)} custom-call(f32[2,4,4,128,128]{4,3,2,1,0:T(8,128)S(1)} %bitcast.10, f32[2,32,128]{2,1,0:T(8,128)S(1)} %get-tuple-element.17.ml_ref, bf16[256,2048]{1,0:T(8,128)(2,1)S(1)} %get-tuple-element.18.wo_ref), custom_call_target="tpu_custom_call" | custom-call | tf_op jit(solution)/shard_map/combine/pallas_call | solution.py:440
  67.9 1.2 %copy.16 = bf16[32,16,8,128]{3,2,0,1:T(8,128)(2,1)} copy(bf16[32,16,8,128]{3,2,1,0:T(8,128)(2,1)S(1)} %bitcast.9) | data formatting | bytes 2097152 | tf_op jit(solution)/shard_map/reshape | solution.py:454
Async XLA Ops:
  0.6 12.0 %copy-start = (s32[128]{0:T(128)S(1)}, s32[128]{0:T(128)}, u32[]{:S(2)}) copy-start(s32[128]{0:T(128)} %pos.1) | copy-start | bytes 1540

commit v4 on v3

--- a/solution.py
+++ b/solution.py
@@ -264,17 +264,21 @@
     lo, hi = pl.ds(0, half), pl.ds(half, half)
     g.greet()
     g.greeted()
-    order = sorted(range(a - 1), key=lambda r: -min(r + 1, a - 1 - r)) + [a - 1]
-
-    ml_cp = remote(ml_ref, ml0, send0.at[2 * a], recv0.at[2 * a], g.partner())
-    ml_cp.start()
+    order = sorted(range(1, a), key=lambda r: -min(r, a - r)) + [0]
+    started = []
+
+    def go_copy(src, dst, send, recv, dev):
+        cp = remote(src, dst, send, recv, dev)
+        cp.start()
+        started.append(cp)
+        return cp
+
+    ml_cp = go_copy(ml_ref, ml0, send0.at[2 * a], recv0.at[2 * a], g.partner())
     core_a, core_b = {}, {}
     for r in order:
-        hy, hx = g.y_at(r + 1), g.x_at(r + 1)
-        core_a[r] = remote(o_ref.at[1 - g.c, hy, :, lo], r0.at[hy, :, lo], send0.at[r], recv0.at[r], g.partner())
-        core_b[r] = remote(o_ref.at[1 - g.c, :, hx, hi], r0.at[:, hx, hi], send0.at[a + r], recv0.at[a + r], g.partner())
-        core_a[r].start()
-        core_b[r].start()
+        hy, hx = g.y_at(r), g.x_at(r)
+        core_a[r] = go_copy(o_ref.at[1 - g.c, hy, :, lo], r0.at[hy, :, lo], send0.at[r], recv0.at[r], g.partner())
+        core_b[r] = go_copy(o_ref.at[1 - g.c, :, hx, hi], r0.at[:, hx, hi], send0.at[a + r], recv0.at[a + r], g.partner())
     ml_cp.wait_recv()
     own = pl.ds(pl.multiple_of(g.c * a * a, a * a), a * a)
     top, fs, total = merge([ml_ref[0, own, :], ml0[0, own, :]], [ml_ref[1, own, :], ml0[1, own, :]])
@@ -286,107 +290,97 @@
             da[i, dst, :] = rows[k, pl.ds(i * a, a), :]
             db[i, dst, :] = rows[k, pl.ds(i, a, stride=a), :]
 
-    ring1 = []
+    ml1, ring1 = {}, {}
+
+    def send_heads(r, qs):
+        hy, hx = g.y_at(r), g.x_at(r)
+        for q in qs:
+            ring1[0, r, q] = go_copy(r0.at[hy, g.x_at(q), lo], r1a.at[r - 1, q], send1.at[0, r, q], recv1.at[0, r, q], g.y_peer(r))
+            ring1[1, r, q] = go_copy(r0.at[g.y_at(q), hx, hi], r1b.at[r - 1, q], send1.at[1, r, q], recv1.at[1, r, q], g.x_peer(r))
+
     for r in order:
-        hy, hx = g.y_at(r + 1), g.x_at(r + 1)
+        hy, hx = g.y_at(r), g.x_at(r)
+        if r:
+            ml1[0, r] = go_copy(mla.at[hy], rmla.at[r - 1], send1.at[2, r, 0], recv1.at[2, r, 0], g.y_peer(r))
+            ml1[1, r] = go_copy(mlb.at[hx], rmlb.at[r - 1], send1.at[2, r, 1], recv1.at[2, r, 1], g.x_peer(r))
         core_a[r].wait_recv()
         ft = fa[hy].T[:half]
         for j in range(a):
             r0[hy, j, lo] = o_ref[g.c, hy, j, lo] * ft[:, j:j + 1] + r0[hy, j, lo] * ft[:, a + j:a + j + 1]
-        if r < a - 1:
-            ring1 += [
-                remote(mla.at[hy], rmla.at[r], send1.at[0, r], recv1.at[0, r], g.y_peer(r + 1)),
-                remote(r0.at[hy, :, lo], r1a.at[r], send1.at[1, r], recv1.at[1, r], g.y_peer(r + 1)),
-            ]
-            ring1[-2].start()
-            ring1[-1].start()
         core_b[r].wait_recv()
         ft = fb[hx].T[half:]
         for j in range(a):
             r0[j, hx, hi] = o_ref[g.c, j, hx, hi] * ft[:, j:j + 1] + r0[j, hx, hi] * ft[:, a + j:a + j + 1]
-        if r < a - 1:
-            ring1 += [
-                remote(mlb.at[hx], rmlb.at[r], send1.at[2, r], recv1.at[2, r], g.x_peer(r + 1)),
-                remote(r0.at[:, hx, hi], r1b.at[r], send1.at[3, r], recv1.at[3, r], g.x_peer(r + 1)),
-            ]
-            ring1[-2].start()
-            ring1[-1].start()
-    for cp in ring1:
+        if r:
+            send_heads(r, order[:2])
+    for r in order[:-1]:
+        send_heads(r, order[2:])
+    for cp in ml1.values():
         cp.wait_recv()
 
-    for side, (ml_own, ml_got, dst, sm) in enumerate(((mla, rmla, s2a, sm2a), (mlb, rmlb, s2b, sm2b))):
-        place = g.x if side else g.y
-        parts = [ml_own.at[place]] + [ml_got.at[r] for r in range(a - 1)]
-        top, fs, total = merge([p[pl.ds(0, a), :] for p in parts], [p[pl.ds(a, a), :] for p in parts])
-        for s in range(a):
-            fcol[pl.ds(s * a, a), :] = fs[s]
-        rows[0, pl.ds(0, a), :] = top
-        rows[1, pl.ds(0, a), :] = total
-        ft = fcol[...].T[half * side:half * (side + 1)]
-        for j in range(a):
-            sm[j, 0:1, :] = rows[0, j:j + 1, :]
-            sm[j, 1:2, :] = rows[1, j:j + 1, :]
-            acc = (r0[j, g.x, hi] if side else r0[g.y, j, lo]) * ft[:, j:j + 1]
-            for r in range(a - 1):
-                got = r1b[r, j] if side else r1a[r, j]
-                acc = acc + got * ft[:, (r + 1) * a + j:(r + 1) * a + j + 1]
-            dst[j] = acc
-
     ring2 = []
-    for r in order[:-1]:
-        hy, hx = g.y_at(r + 1), g.x_at(r + 1)
-        ring2 += [
-            remote(sm2a.at[hx], rm2a.at[r], send2.at[0, r], recv2.at[0, r], g.x_peer(r + 1)),
-            remote(s2a.at[hx], r2a.at[r], send2.at[1, r], recv2.at[1, r], g.x_peer(r + 1)),
-            remote(sm2b.at[hy], rm2b.at[r], send2.at[2, r], recv2.at[2, r], g.y_peer(r + 1)),
-            remote(s2b.at[hy], r2b.at[r], send2.at[3, r], recv2.at[3, r], g.y_peer(r + 1)),
-        ]
-    for cp in ring2:
-        cp.start()
+    for i, q in enumerate(order):
+        hy, hx = g.y_at(q), g.x_at(q)
+        for side, (ml_own, ml_got, dst, sm) in enumerate(((mla, rmla, s2a, sm2a), (mlb, rmlb, s2b, sm2b))):
+            head = hy if side else hx
+            parts = [ml_own.at[g.x if side else g.y]] + [ml_got.at[r - 1] for r in range(1, a)]
+            top, fs, total = merge([p[pl.ds(head, 1), :] for p in parts], [p[pl.ds(a + head, 1), :] for p in parts])
+            fc = fcol.at[2 * i + side]
+            for s in range(a):
+                fc[s:s + 1, :] = fs[s]
+            sm[head, 0:1, :] = top
+            sm[head, 1:2, :] = total
+            ft = fc[...].T[half * side:half * (side + 1)]
+            acc = (r0[head, g.x, hi] if side else r0[g.y, head, lo]) * ft[:, 0:1]
+            for r in range(1, a):
+                ring1[side, r, q].wait_recv()
+            for r in range(1, a):
+                acc = acc + (r1b if side else r1a)[r - 1, q] * ft[:, r:r + 1]
+            dst[head] = acc
+            if q:
+                rm, r2 = (rm2b, r2b) if side else (rm2a, r2a)
+                peer = g.y_peer(q) if side else g.x_peer(q)
+                ring2.append(go_copy(sm.at[head], rm.at[q - 1], send2.at[2 * side, q], recv2.at[2 * side, q], peer))
+                ring2.append(go_copy(dst.at[head], r2.at[q - 1], send2.at[2 * side + 1, q], recv2.at[2 * side + 1, q], peer))
     for cp in ring2:
         cp.wait_recv()
     for side, (sm, rm, mine, got) in enumerate(((sm2a, rm2a, s2a, r2a), (sm2b, rm2b, s2b, r2b))):
         place = g.y if side else g.x
         parts = [sm.at[place]] + [rm.at[r] for r in range(a - 1)]
         top, fs, total = merge([p[0:1, :] for p in parts], [p[1:2, :] for p in parts])
+        fc = fcol.at[2 * a + side]
         for s in range(a):
-            fcol[pl.ds(s, 1), :] = fs[s]
-        fcol[pl.ds(a, 1), :] = total
-        ft = fcol[...].T[half * side:half * (side + 1)]
+            fc[s:s + 1, :] = fs[s]
+        fc[a:a + 1, :] = total
+        ft = fc[...].T[half * side:half * (side + 1)]
         acc = mine[place] * ft[:, 0:1]
         for r in range(a - 1):
             acc = acc + got[r] * ft[:, r + 1:r + 2]
         go[g.c, (hi if side else lo), :] = (acc / ft[:, a:a + 1]).astype(BF16)
 
-    heads = remote(go.at[g.c], go.at[g.c], osem.at[0], osem.at[1], g.partner())
-    heads.start()
-    heads.wait_recv()
+    go_copy(go.at[g.c], go.at[g.c], osem.at[0], osem.at[1], g.partner()).wait_recv()
     lhs = jnp.concatenate([go[0], go[1]], axis=1)
     for i in range(a):
         part = jnp.dot(lhs, wo_ref[:, pl.ds(i * a * hd, a * hd)], preferred_element_type=F32)
         for j in range(a):
             r0y[i, j] = part[:, j * hd:(j + 1) * hd]
-    ring3, ring4 = [], []
-    for r in order[:-1]:
-        hy, hx = g.y_at(r + 1), g.x_at(r + 1)
-        ring3 += [
-            remote(r0y.at[hy, :, lo], y1a.at[r], send3.at[0, r], recv3.at[0, r], g.y_peer(r + 1)),
-            remote(r0y.at[:, hx, hi], y1b.at[r], send3.at[1, r], recv3.at[1, r], g.x_peer(r + 1)),
-        ]
-    for cp in ring3:
-        cp.start()
-    for cp in ring3:
-        cp.wait_recv()
-    t2a[...] = functools.reduce(jnp.add, [y1a[r] for r in range(a - 1)], r0y[g.y, :, lo])
-    t2b[...] = functools.reduce(jnp.add, [y1b[r] for r in range(a - 1)], r0y[:, g.x, hi])
-    for r in order[:-1]:
-        hy, hx = g.y_at(r + 1), g.x_at(r + 1)
-        ring4 += [
-            remote(t2a.at[hx], y2a.at[r], send4.at[0, r], recv4.at[0, r], g.x_peer(r + 1)),
-            remote(t2b.at[hy], y2b.at[r], send4.at[1, r], recv4.at[1, r], g.y_peer(r + 1)),
-        ]
-    for cp in ring4:
-        cp.start()
+    ring3, ring4 = {}, []
+    for q in order:
+        for r in order[:-1]:
+            hy, hx = g.y_at(r), g.x_at(r)
+            ring3[0, r, q] = go_copy(r0y.at[hy, g.x_at(q), lo], y1a.at[r - 1, q], send3.at[0, r, q], recv3.at[0, r, q], g.y_peer(r))
+            ring3[1, r, q] = go_copy(r0y.at[g.y_at(q), hx, hi], y1b.at[r - 1, q], send3.at[1, r, q], recv3.at[1, r, q], g.x_peer(r))
+    for q in order:
+        hy, hx = g.y_at(q), g.x_at(q)
+        for side in range(2):
+            for r in range(1, a):
+                ring3[side, r, q].wait_recv()
+            got = y1b if side else y1a
+            mine = r0y[hy, g.x, hi] if side else r0y[g.y, hx, lo]
+            dst = t2b.at[hy] if side else t2a.at[hx]
+            dst[...] = functools.reduce(jnp.add, [got[r - 1, q] for r in range(1, a)], mine)
+            if q:
+                ring4.append(go_copy(dst, (y2b if side else y2a).at[q - 1], send4.at[side, q], recv4.at[side, q], g.y_peer(q) if side else g.x_peer(q)))
     for cp in ring4:
         cp.wait_recv()
     y_out[g.c, g.y, g.x, lo, :] = functools.reduce(jnp.add, [y2a[r] for r in range(a - 1)], t2a[g.x]).astype(BF16)
@@ -394,7 +388,7 @@
     outs = Gather(g, y_out, bsend, brecv)
     outs.start()
     outs.finish()
-    for cp in [ml_cp, heads] + list(core_a.values()) + list(core_b.values()) + ring1 + ring2 + ring3 + ring4:
+    for cp in started:
         cp.wait_send()
 
 
@@ -443,11 +437,11 @@
             in_specs=[vmem] * 3,
             out_specs=vmem,
             scratch_shapes=[f32(a, a, n_rows, hd), f32(2, n, n_rows), f32(4, a * a, n_rows)]
-            + [f32(a, 2 * a, n_rows)] * 2 + [f32(max(a * a, 8), n_rows)] + [f32(a, 2 * a, n_rows)] * 2
+            + [f32(a, 2 * a, n_rows)] * 2 + [f32(2 * a + 2, 8, n_rows)] + [f32(a, 2 * a, n_rows)] * 2
             + [f32(a - 1, a, half, hd)] * 2 + [f32(a - 1, 2 * a, n_rows)] * 2
             + [f32(a, half, hd)] * 2 + [f32(a, 8, n_rows)] * 2 + [f32(a - 1, half, hd)] * 2 + [f32(a - 1, 8, n_rows)] * 2
             + [bf16(2, n_rows, hd), f32(a, a, n_rows, hd)] + [f32(a - 1, a, half, hd)] * 2 + [f32(a, half, hd)] * 2 + [f32(a - 1, half, hd)] * 2
-            + [dma((2 * a + 1,))] * 2 + [dma((4, a - 1))] * 4 + [dma((2,))] + [dma((2, a - 1))] * 4 + sems,
+            + [dma((2 * a + 1,))] * 2 + [dma((3, a, a))] * 2 + [dma((4, a))] * 2 + [dma((2,))] + [dma((2, a, a))] * 2 + [dma((2, a))] * 2 + sems,
             compiler_params=pltpu.CompilerParams(collective_id=1, has_side_effects=True, vmem_limit_bytes=16 << 20),
             name='combine',
         )(o.reshape(2, a, a, n_rows, hd), ml, wo)

time: 69.2 us -> 66.2 us (0.957)
  Pallas kernels: 67.2 us -> 64.2 us
    pallas_call x1, Pallas kernels: 46.9 us -> 43.9 us  [local_step(): pl.pallas_call(functools.partial(combine_kernel, n), out_shape=shape((2,...]
where the time goes in v4:
time: 66.2 us; the launch traced here: 66.1 us
  Pallas kernels  64.2 us (97%)
  local copies, waits for them, and re-layouts  1.25 us (2%)
  between operations  0.67 us (1%)
    pallas_call x1, Pallas kernels, local_step(): pl.pallas_call(functools.partial(combine_kernel, n), out_shape=shape((2,...  43.9 us
    pallas_call x1, Pallas kernels, local_step(): pl.pallas_call(functools.partial(project_kernel, n), out_shape=(shape((2,...  12 us
    pallas_call x1, Pallas kernels, local_step(): pl.pallas_call(functools.partial(attend_kernel, blk), out_shape=(cache, c...  8.27 us

profile of v4, /device:TPU:97, one launch (start us, length us, event | category | flops | bytes accessed | tf_op | source)
XLA Modules:
  0.0 66.1 jit_solution(230160072126350621)
XLA Ops:
  0.6 0.0 copy-start
  0.6 12.0 %project.1 = (bf16[2,16,128,128]{3,2,1,0:T(8,128)(2,1)S(1)}, f32[2,128,128]{2,1,0:T(8,128)S(1)}, bf16[256,2048]{1,0:T(8,128)(2,1)S(1)}, bf16[128,256,128]{2,1,0:T(8,128)(2,1)S(1)}, bf16[128,256,128]{2,1,0:T(8,128)(2,1)S(1)}) custom-call(bf16[128,4096]{1,0:T(8,128)(2,1)} %x_hbm.1, bf16[4096,4096]{1,0:T(8,128)(2,1)} %wq_hbm.1, bf16[4096,128]{1,0:T(8,128)(2,1)} %wk_hbm.1, ...), custom_call_target="tpu_custom_call" | custom-call | tf_op jit(solution)/shard_map/project/pallas_call | solution.py:415
  12.7 0.0 copy-done
  12.7 8.3 %attend.1 = (bf16[128,256,128]{2,1,0:T(8,128)(2,1)}, bf16[128,256,128]{2,1,0:T(8,128)(2,1)}, f32[4096,128]{1,0:T(8,128)S(1)}, f32[2,32,128]{2,1,0:T(8,128)S(1)},...) custom-call(s32[128]{0:T(128)S(1)} %copy-done, ...), custom_call_target="tpu_custom_call", output_to_operand_aliasing={{4}: (3, {}), {5}: (4, {})} | custom-call | tf_op jit(solution)/shard_map/attend/pallas_call | solution.py:424
  20.9 43.9 %combine.1 = bf16[2,4,4,128,128]{4,3,2,1,0:T(8,128)(2,1)S(1)} custom-call(f32[2,4,4,128,128]{4,3,2,1,0:T(8,128)S(1)} %bitcast.10, f32[2,32,128]{2,1,0:T(8,128)S(1)} %get-tuple-element.17.ml_ref, bf16[256,2048]{1,0:T(8,128)(2,1)S(1)} %get-tuple-element.18.wo_ref), custom_call_target="tpu_custom_call" | custom-call | tf_op jit(solution)/shard_map/combine/pallas_call | solution.py:434
  64.9 1.2 %copy.16 = bf16[32,16,8,128]{3,2,0,1:T(8,128)(2,1)} copy(bf16[32,16,8,128]{3,2,1,0:T(8,128)(2,1)S(1)} %bitcast.9) | data formatting | bytes 2097152 | tf_op jit(solution)/shard_map/reshape | solution.py:448
Async XLA Ops:
  0.6 12.0 %copy-start = (s32[128]{0:T(128)S(1)}, s32[128]{0:T(128)}, u32[]{:S(2)}) copy-start(s32[128]{0:T(128)} %pos.1) | copy-start | bytes 1540
